TPU v7x, 32 devices: a whole 2x2x4 slice. The times are simulated.
32 devices in a mesh: dom: 32 (over z, y, x, core).
Axes of the slice: x: 2, y: 2, z: 4, core: 2. Of those that a mesh axis runs over, the one named last changes fastest.
Arguments:
- forcing: float32 [1024, 128], P('dom'), may hold values from -6 to 6
- first_guess: float32 [1024, 128], P('dom'), may hold values from -4 to 4
- corners: int32 [3, 262144], P(None, 'dom'), may hold values from 0 to 8191, as said below
- gradients: float32 [4, 262144], P(None, 'dom'), may hold values from -5 to 5
- element_area: float32 [262144], P('dom'), may hold values from 0.5 to 2
- element_depth: float32 [262144], P('dom'), may hold values from 0.2 to 4
- send_blocks: int32 [32, 4, 8], P('dom'), may hold values from 0 to 32, as said below
- recv_blocks: int32 [32, 4, 8], P('dom'), may hold values from 0 to 32, as said below
Outputs:
- elevation: float32 [1024, 128], P('dom')
- residual_left: float32 [1024, 128], P('dom')
Inputs may be any that keep to these rules, and one draw needn't show every extreme that they name: `corners`: column e of device d's elements names three different local nodes of device d, numbered below (64) * 128: numbers below 4096 are its owned nodes in block order, the rest its halo blocks. The first corner is an owned node, and every owned node is the first corner of some element of its device. `send_blocks`: entry [d, o, s] is the owned block of device d sent in slot s of offset o to the reader d - k_o, or 32 for an empty slot; it is live exactly when recv_blocks[d - k_o, o, s] is, and readers outside the mesh get nothing. Live blocks of one device and offset differ. For k_o = 1 every slot toward an existing reader is live. `recv_blocks`: entry [q, o, s] is the halo block of device q filled by slot s of offset o from device q + k_o, or 32 for an empty slot. The live entries of one device differ.
All inputs are finite; a program needn't handle non-finite values.
Results may differ from a plain program's by a relative error of at most 0.00022.
Values sent between devices are 32-bit elements; how exact they have to be, the bound alone decides.
A program may use at most 64 MiB of HBM per device.

v0:
```python
import functools

import jax
import jax.numpy as jnp
from jax import lax
from jax.experimental import pallas as pl
from jax.experimental.pallas import tpu as pltpu
from jax.sharding import PartitionSpec as P

LANES = 128
ROWS = 8
WIDE = 4


def shift_list(offsets):
    half_count = offsets // 2
    return [
        shift_at - half_count if shift_at < half_count else shift_at - half_count + 1
        for shift_at in range(offsets)
    ]


def learning_rounds(n, reach):
    rounds = []
    while reach < n - 1:
        rounds.append(reach)
        reach *= 2
    return rounds


def kernel(
    n,
    forcing,
    guess,
    corners,
    gradients,
    area,
    depth,
    send,
    recv,
    both,
    blk,
    lane,
    hot,
    elem,
    vals,
    hi,
    lo,
    field,
    halo_part,
    fwd_out,
    fwd_in,
    bwd_out,
    bwd_in,
    sum_out,
    sum_in,
    fwd_send_sem,
    fwd_recv_sem,
    bwd_send_sem,
    bwd_recv_sem,
    sum_send_sem,
    sum_recv_sem,
    known,
):
    own, _ = forcing.shape
    _, offsets, slots = send.shape
    halo = offsets * slots
    rows = area.shape[0]
    groups = rows // ROWS
    shifts = shift_list(offsets)
    me = lax.axis_index("dom")
    f32 = jnp.float32

    def there(distance):
        return jnp.logical_and(me + distance >= 0, me + distance < n)

    def fwd_copy(t, o):
        return pltpu.make_async_remote_copy(
            src_ref=fwd_out.at[t, o],
            dst_ref=fwd_in.at[t, o],
            send_sem=fwd_send_sem.at[t, o],
            recv_sem=fwd_recv_sem.at[t, o],
            device_id=(me - shifts[o],),
            device_id_type=pl.DeviceIdType.MESH,
        )

    def bwd_copy(t, o):
        return pltpu.make_async_remote_copy(
            src_ref=bwd_out.at[t, o],
            dst_ref=bwd_in.at[t, o],
            send_sem=bwd_send_sem.at[t, o],
            recv_sem=bwd_recv_sem.at[t, o],
            device_id=(me + shifts[o],),
            device_id_type=pl.DeviceIdType.MESH,
        )

    def when_there(distance, action):
        @pl.when(there(distance))
        def _():
            action()

    barrier = pltpu.get_barrier_semaphore()
    reach = max(shifts)
    near = [shift for shift in range(-reach, reach + 1) if shift != 0]
    for shift in near:
        when_there(
            shift,
            lambda shift=shift: pl.semaphore_signal(
                barrier,
                inc=1,
                device_id=(me + shift,),
                device_id_type=pl.DeviceIdType.MESH,
            ),
        )

    rounds = learning_rounds(n, reach)

    def tell(i):
        for side in range(2):
            far = rounds[i] * (2 * side - 1)
            when_there(
                far,
                lambda side=side, far=far: pl.semaphore_signal(
                    known.at[i, side],
                    inc=1,
                    device_id=(me + far,),
                    device_id_type=pl.DeviceIdType.MESH,
                ),
            )

    def learn(i):
        for side in range(2):
            far = rounds[i] * (1 - 2 * side)
            when_there(
                far, lambda side=side: pl.semaphore_wait(known.at[i, side], 1)
            )

    def next_round(i):
        if i > 0 and i <= len(rounds):
            learn(i - 1)
        if i < len(rounds):
            tell(i)

    for o in range(offsets):

        @pl.when(jnp.logical_not(there(shifts[o])))
        def _():
            for t in range(3):
                fwd_in[t, o] = jnp.zeros((slots, LANES), f32)

        @pl.when(jnp.logical_not(there(-shifts[o])))
        def _():
            for t in range(3):
                bwd_in[t, o] = jnp.zeros((slots, LANES), f32)

    def pack(t, source):
        for o in range(offsets):
            for s in range(slots):
                at = jnp.minimum(send[0, o, s], own - 1)
                fwd_out[t, o, s : s + 1, :] = source[pl.ds(at, 1), :]

    def start_forward(t):
        for o in range(offsets):
            when_there(-shifts[o], lambda o=o: fwd_copy(t, o).start())

    def lay(r, carry):
        at = pl.multiple_of(r * LANES, LANES)
        for c in range(3):
            lane[pl.ds(c * rows + r, 1), :] = corners[c : c + 1, pl.ds(at, LANES)]
        for c in range(4):
            elem[pl.ds(c * rows + r, 1), :] = gradients[c : c + 1, pl.ds(at, LANES)]
        return carry

    lax.fori_loop(0, rows, lay, 0)

    wide = lax.broadcasted_iota(jnp.int32, (ROWS, LANES), 1)
    table = jnp.where(wide < own, wide, 2 * LANES)
    for o in range(offsets):
        for s in range(slots):
            table = jnp.where(wide == own + recv[0, o, s], own + o * slots + s, table)
    table = jnp.where(wide < own + halo, table, 2 * LANES)

    def number(g, carry):
        at = pl.multiple_of(g * ROWS, ROWS)
        node = lane[pl.ds(at, ROWS), :]
        block = lax.shift_right_logical(node, 7)
        blk[pl.ds(at, ROWS), :] = jnp.take_along_axis(
            table, block, axis=1, mode="promise_in_bounds"
        )
        lane[pl.ds(at, ROWS), :] = lax.bitwise_and(node, LANES - 1)
        return carry

    lax.fori_loop(0, 3 * groups, number, 0)

    tall = lax.broadcasted_iota(jnp.int32, (LANES, LANES), 0)

    def heat(g, carry):
        at = pl.multiple_of(g * ROWS, ROWS)
        for j in range(ROWS):
            row = lane[pl.ds(at + j, 1), :]
            hot[pl.ds(pl.multiple_of((at + j) * LANES, LANES), LANES), :] = (
                jnp.where(row == tall, 1.0, 0.0).T.astype(jnp.bfloat16)
            )
        return carry

    lax.fori_loop(groups, 2 * groups, heat, 0)
    pack(0, guess)
    pl.semaphore_wait(
        barrier, jnp.minimum(me, reach) + jnp.minimum(n - 1 - me, reach)
    )
    start_forward(0)
    next_round(0)
    lax.fori_loop(2 * groups, 3 * groups, heat, 0)

    def picked(source, count, first, value, index, block):
        for b in range(count):
            row = jnp.broadcast_to(source(b), (ROWS, LANES))
            got = jnp.take_along_axis(row, index, axis=1, mode="promise_in_bounds")
            value = jnp.where(block == first + b, got, value)
        return value

    def operate(t, source, between, after, finished):
        def gather_own(g, carry):
            for j in range(WIDE):
                at = pl.multiple_of((g * WIDE + j) * ROWS, ROWS)
                vals[t // 2, pl.ds(at, ROWS), :] = picked(
                    lambda b: source[b : b + 1, :],
                    own,
                    0,
                    jnp.zeros((ROWS, LANES), f32),
                    lane[pl.ds(at, ROWS), :],
                    blk[pl.ds(at, ROWS), :],
                )
            return carry

        lax.fori_loop(0, 3 * groups // WIDE, gather_own, 0)
        for o in range(offsets):
            when_there(shifts[o], lambda o=o: fwd_copy(t, o).wait_recv())

        step = finished()

        def one_group(g, energy):
            at = pl.multiple_of(g * ROWS, ROWS)
            u = [vals[t // 2, pl.ds(at, ROWS), :]]
            for c in (1, 2):
                here = pl.multiple_of(c * rows + at, ROWS)
                u.append(
                    picked(
                        lambda b: fwd_in[t, b // slots, b % slots : b % slots + 1, :],
                        halo,
                        own,
                        vals[t // 2, pl.ds(here, ROWS), :],
                        lane[pl.ds(here, ROWS), :],
                        blk[pl.ds(here, ROWS), :],
                    )
                )
                if t == 1:
                    vals[0, pl.ds(here, ROWS), :] = u[c]
            if t == 2:
                for c in range(3):
                    here = pl.multiple_of(c * rows + at, ROWS)
                    u[c] = vals[0, pl.ds(here, ROWS), :] - step * u[c]
            gx0, gy0, gx1, gy1 = [
                elem[pl.ds(pl.multiple_of(c * rows + at, ROWS), ROWS), :] for c in range(4)
            ]
            size = area[pl.ds(at, ROWS), :]
            scaled = depth[pl.ds(at, ROWS), :] * size
            third = size / 3.0
            from0, from1 = u[0] - u[2], u[1] - u[2]
            slope_x = scaled * (gx0 * from0 + gx1 * from1)
            slope_y = scaled * (gy0 * from0 + gy1 * from1)
            flow0 = gx0 * slope_x + gy0 * slope_y
            flow1 = gx1 * slope_x + gy1 * slope_y
            adds = [
                flow0 + third * u[0],
                flow1 + third * u[1],
                third * u[2] - (flow0 + flow1),
            ]
            for c in range(3):
                here = pl.multiple_of(c * rows + at, ROWS)
                top = adds[c].astype(jnp.bfloat16).astype(f32)
                hi[pl.ds(here, ROWS), :] = top
                lo[pl.ds(here, ROWS), :] = adds[c] - top
            return energy + (
                slope_x * (gx0 * from0 + gx1 * from1)
                + slope_y * (gy0 * from0 + gy1 * from1)
                + third * (u[0] * u[0] + u[1] * u[1] + u[2] * u[2])
            )

        def gather_halo(g, energy):
            for j in range(2):
                energy = one_group(g * 2 + j, energy)
            return energy

        energy = lax.fori_loop(0, groups // 2, gather_halo, jnp.zeros((ROWS, LANES), f32))
        between(energy)

        def summed(first_group, last_group, count, first):
            names = first + lax.broadcasted_iota(jnp.int32, (count, LANES), 0)

            def body(g, acc):
                at = pl.multiple_of(g * WIDE * ROWS, ROWS)
                parts = []
                for j in range(WIDE * ROWS):
                    mask = blk[pl.ds(at + j, 1), :] == names
                    parts.append(
                        jnp.concatenate(
                            [
                                jnp.where(mask, hi[pl.ds(at + j, 1), :], 0.0),
                                jnp.where(mask, lo[pl.ds(at + j, 1), :], 0.0),
                            ],
                            axis=0,
                        ).astype(jnp.bfloat16)
                    )
                left = jnp.concatenate(parts, axis=1)
                right = hot[pl.ds(pl.multiple_of(at * LANES, LANES), WIDE * ROWS * LANES), :]
                return acc + jnp.dot(left, right, preferred_element_type=f32)

            acc = lax.fori_loop(
                first_group // WIDE, last_group // WIDE, body, jnp.zeros((2 * count, LANES), f32)
            )
            return acc[:count] + acc[count:]

        if t == 0:
            next_round(1)
        halo_sum = summed(groups, 3 * groups, halo, own)
        for o in range(offsets):
            bwd_out[t, o] = halo_sum[o * slots : (o + 1) * slots]
        for o in range(offsets):
            when_there(shifts[o], lambda o=o: bwd_copy(t, o).start())
        after()
        if t == 0:
            next_round(2)
            lax.fori_loop(0, groups, heat, 0)
        total = summed(0, 3 * groups, own, 0)
        for o in range(offsets):
            when_there(-shifts[o], lambda o=o: bwd_copy(t, o).wait_recv())
        names = lax.broadcasted_iota(jnp.int32, (own, LANES), 0)
        for o in range(offsets):
            for s in range(slots):
                total = total + jnp.where(
                    names == send[0, o, s], bwd_in[t, o, s : s + 1, :], 0.0
                )
        return total

    small = lax.broadcasted_iota(jnp.int32, (1, LANES), 1)

    def whole(a):
        return jnp.sum(jnp.sum(a, axis=0, keepdims=True), axis=1, keepdims=True)

    def start_sum(k, terms):
        line = jnp.zeros((1, LANES), f32)
        for i, term in enumerate(terms):
            line = jnp.where(small == i, whole(term), line)
        sum_out[k] = line
        sum_in[k, me] = line

        def push(i, carry):
            pltpu.make_async_remote_copy(
                src_ref=sum_out.at[k],
                dst_ref=sum_in.at[k, me],
                send_sem=sum_send_sem.at[k],
                recv_sem=sum_recv_sem.at[k],
                device_id=(lax.rem(me + i, n),),
                device_id_type=pl.DeviceIdType.MESH,
            ).start()
            return carry

        lax.fori_loop(1, n, push, 0)

    def sum_bytes(k):
        return sum_in.at[k, pl.ds(0, n - 1)]

    def finish_sum(k, count):
        pltpu.make_async_copy(sum_bytes(k), sum_bytes(k), sum_recv_sem.at[k]).wait()
        line = jnp.sum(sum_in[k], axis=0)
        return [
            jnp.sum(jnp.where(small == i, line, 0.0), axis=1, keepdims=True)
            for i in range(count)
        ]

    def nothing(*_):
        return None

    field[0] = forcing[...] - operate(0, guess, nothing, nothing, nothing)
    pack(1, field.at[0])
    start_forward(1)
    next_round(3)
    for i in range(4, len(rounds) + 1):
        next_round(i)
    energies = []

    def first_sums():
        start_sum(0, [field[0] * field[0], energies[0]])

    field[2] = operate(1, field.at[0], energies.append, first_sums, nothing)
    pack(2, field.at[2])
    start_forward(2)
    sums = []

    def first_step():
        norm, crossed = finish_sum(0, 2)
        step = norm / crossed
        sums.extend([norm, crossed, step])
        field[1] = field[0] - step * field[2]
        return step

    def second_sums(energy):
        start_sum(1, [field[1] * field[1], energy, field[1] * field[2]])

    applied = operate(2, field.at[2], second_sums, nothing, first_step)
    norm, crossed, step = sums
    for t in range(3):
        for o in range(offsets):
            when_there(-shifts[o], lambda t=t, o=o: fwd_copy(t, o).wait_send())
            when_there(shifts[o], lambda t=t, o=o: bwd_copy(t, o).wait_send())
    fresh, own_pair, mixed = finish_sum(1, 3)
    beta = fresh / norm
    next_step = fresh / (own_pair + beta * (2.0 * mixed + beta * crossed))
    both[0:own] = guess[...] + step * field[0] + next_step * (field[1] + beta * field[0])
    both[own : 2 * own] = field[1] - next_step * (applied + beta * field[2])
    for k in range(2):
        pltpu.make_async_copy(sum_bytes(k), sum_bytes(k), sum_send_sem.at[k]).wait()


def local(
    n,
    forcing,
    first_guess,
    corners,
    gradients,
    element_area,
    element_depth,
    send_blocks,
    recv_blocks,
):
    own, columns = forcing.shape
    _, offsets, slots = send_blocks.shape
    count = element_area.shape[0]
    rows = count // LANES
    assert columns == LANES and own + offsets * slots <= LANES and rows % (ROWS * WIDE) == 0
    f32 = jnp.float32
    vmem = pl.BlockSpec(memory_space=pltpu.VMEM)
    smem = pl.BlockSpec(memory_space=pltpu.SMEM)
    dma = pltpu.SemaphoreType.DMA
    part = (3, offsets, slots, LANES)
    both = pl.pallas_call(
        functools.partial(kernel, n),
        out_shape=jax.ShapeDtypeStruct((2 * own, columns), f32),
        in_specs=[vmem] * 6 + [smem] * 2,
        out_specs=vmem,
        scratch_shapes=[
            pltpu.VMEM((3 * rows, LANES), jnp.int32),
            pltpu.VMEM((3 * rows, LANES), jnp.int32),
            pltpu.VMEM((3 * count, LANES), jnp.bfloat16),
            pltpu.VMEM((4 * rows, LANES), f32),
            pltpu.VMEM((2, 3 * rows, LANES), f32),
            pltpu.VMEM((3 * rows, LANES), f32),
            pltpu.VMEM((3 * rows, LANES), f32),
            pltpu.VMEM((3, own, LANES), f32),
            pltpu.VMEM((offsets * slots, LANES), f32),
            pltpu.VMEM(part, f32),
            pltpu.VMEM(part, f32),
            pltpu.VMEM(part, f32),
            pltpu.VMEM(part, f32),
            pltpu.VMEM((2, 1, LANES), f32),
            pltpu.VMEM((2, n, 1, LANES), f32),
            dma((3, offsets)),
            dma((3, offsets)),
            dma((3, offsets)),
            dma((3, offsets)),
            dma((2,)),
            dma((2,)),
            pltpu.SemaphoreType.REGULAR((len(learning_rounds(n, max(shift_list(offsets)))) + 1, 2)),
        ],
        compiler_params=pltpu.CompilerParams(collective_id=0, has_side_effects=True),
    )(
        forcing,
        first_guess,
        corners,
        gradients,
        element_area.reshape(rows, LANES),
        element_depth.reshape(rows, LANES),
        send_blocks,
        recv_blocks,
    )
    return both[:own], both[own:]


def solution(mesh):
    placed = (
        P("dom", None),
        P("dom", None),
        P(None, "dom"),
        P(None, "dom"),
        P("dom"),
        P("dom"),
        P("dom", None, None),
        P("dom", None, None),
    )
    return jax.shard_map(
        functools.partial(local, mesh.shape["dom"]),
        mesh=mesh,
        in_specs=placed,
        out_specs=(P("dom", None), P("dom", None)),
        check_vma=False,
    )
```

profile of v0, /device:TPU:0, one launch (start us, length us, event | category | flops | bytes accessed | tf_op | source)
XLA Modules:
  0.0 38.3 jit_solution(17457225126419254873)
XLA Ops:
  0.6 36.3 %shard_map.95 = f32[64,128]{1,0:T(8,128)} custom-call(f32[32,128]{1,0:T(8,128)} %forcing.1, f32[32,128]{1,0:T(8,128)} %guess.1, s32[3,8192]{1,0:T(4,128)} %corners.1, f32[4,8192]{1,0:T(4,128)} %gradients.1, f32[64,128]{1,0:T(8,128)} %bitcast.2, f32[64,128]{1,0:T(8,128)} %bitcast.3, s32[1,4,8]{2,1,0:T(4,128)} %send.1, s32[1,4,8]{2,1,0:T(4,128)} %recv.1), custom_call_target="tpu_custom_call" | custom-call | tf_op jit(solution)/shard_map/pallas_call | solution.py:447
  36.9 1.3 %fusion = (f32[32,128]{1,0:T(8,128)}, f32[32,128]{1,0:T(8,128)}) fusion(f32[64,128]{1,0:T(8,128)} %shard_map.95), kind=kLoop, calls=%fused_computation | loop fusion | bytes 65536 | tf_op jit(solution)/shard_map/slice | solution.py:487
where the time goes:
time: 38.5 us; the launch traced here: 38.3 us
  Pallas kernels  36.3 us (94%)
  local copies, waits for them, and re-layouts  1.35 us (4%)
  between operations  0.64 us (2%)
    pallas_call x1, Pallas kernels, local(): pl.pallas_call(functools.partial(kernel, n), out_shape=jax.ShapeDtypeStru...  36.3 us
    slice x1, local copies, waits for them, and re-layouts, local(): return (both[:own], both[own:])  1.35 us

commit v1 on v0

v1 whole, which is shorter than its diff:
```python
import functools

import jax
import jax.numpy as jnp
from jax import lax
from jax.experimental import pallas as pl
from jax.experimental.pallas import tpu as pltpu
from jax.sharding import PartitionSpec as P

LANES = 128
ROWS = 8
LAY = 8


def shift_list(offsets):
    half_count = offsets // 2
    return [
        shift_at - half_count if shift_at < half_count else shift_at - half_count + 1
        for shift_at in range(offsets)
    ]


def learning_rounds(n, reach):
    rounds = []
    while reach < n - 1:
        rounds.append(reach)
        reach *= 2
    return rounds


def message_pairs(shifts):
    roles = sorted([0, *shifts])
    reach = max(roles) - min(roles)
    return {
        distance: [(a, b) for a in roles for b in roles if a - b == distance]
        for distance in range(-reach, reach + 1)
        if distance != 0
    }


def kernel(
    n,
    forcing,
    guess,
    corners,
    gradients,
    area,
    depth,
    send,
    recv,
    both,
    blk,
    lane,
    hot,
    elem,
    vals,
    hi,
    lo,
    table,
    base,
    links,
    links_in,
    guess_out,
    mix_out,
    mix_in,
    back_out,
    back_in,
    sum_out,
    sum_in,
    guess_send_sem,
    guess_recv_sem,
    link_send_sem,
    link_recv_sem,
    mix_send_sem,
    mix_recv_sem,
    back_send_sem,
    back_recv_sem,
    sum_send_sem,
    sum_recv_sem,
    known,
):
    own, _ = forcing.shape
    _, offsets, slots = send.shape
    halo = offsets * slots
    nodes = own + halo
    rows = area.shape[0]
    groups = rows // ROWS
    shifts = shift_list(offsets)
    pairs = message_pairs(shifts)
    distances = list(pairs)
    reach = max(distances)
    me = lax.axis_index("dom")
    f32 = jnp.float32
    bf16 = jnp.bfloat16

    def there(distance):
        return jnp.logical_and(me + distance >= 0, me + distance < n)

    def when_there(distance, action):
        @pl.when(there(distance))
        def _():
            action()

    def remote(source, target, send_sem, recv_sem, distance):
        return pltpu.make_async_remote_copy(
            src_ref=source,
            dst_ref=target,
            send_sem=send_sem,
            recv_sem=recv_sem,
            device_id=(me + distance,),
            device_id_type=pl.DeviceIdType.MESH,
        )

    def guess_copy(o):
        return remote(
            guess_out.at[o],
            table.at[0, pl.ds(own + o * slots, slots)],
            guess_send_sem.at[o],
            guess_recv_sem.at[o],
            -shifts[o],
        )

    def link_copy(o):
        return remote(
            links, links_in.at[o], link_send_sem.at[o], link_recv_sem.at[o], -shifts[o]
        )

    def mix_copy(e, i):
        count = len(pairs[distances[i]])
        return remote(
            mix_out.at[e, i, pl.ds(0, count)],
            mix_in.at[e, i, pl.ds(0, count)],
            mix_send_sem.at[e, i],
            mix_recv_sem.at[e, i],
            distances[i],
        )

    def back_copy(o):
        return remote(
            back_out.at[o], back_in.at[o], back_send_sem.at[o], back_recv_sem.at[o], shifts[o]
        )

    barrier = pltpu.get_barrier_semaphore()
    for distance in distances:
        when_there(
            distance,
            lambda distance=distance: pl.semaphore_signal(
                barrier,
                inc=1,
                device_id=(me + distance,),
                device_id_type=pl.DeviceIdType.MESH,
            ),
        )

    rounds = learning_rounds(n, reach)

    def tell(i):
        for side in range(2):
            far = rounds[i] * (2 * side - 1)
            when_there(
                far,
                lambda side=side, far=far: pl.semaphore_signal(
                    known.at[i, side],
                    inc=1,
                    device_id=(me + far,),
                    device_id_type=pl.DeviceIdType.MESH,
                ),
            )

    def learn(i):
        for side in range(2):
            far = rounds[i] * (1 - 2 * side)
            when_there(
                far, lambda side=side: pl.semaphore_wait(known.at[i, side], 1)
            )

    def next_round(i):
        if i > 0 and i <= len(rounds):
            learn(i - 1)
        if i < len(rounds):
            tell(i)

    for o in range(offsets):

        @pl.when(jnp.logical_not(there(shifts[o])))
        def _():
            table[0, own + o * slots : own + (o + 1) * slots] = jnp.zeros((slots, LANES), f32)
            links_in[o] = jnp.full((halo, LANES), own, jnp.int32)

        @pl.when(jnp.logical_not(there(-shifts[o])))
        def _():
            back_in[o] = jnp.zeros((slots, LANES), f32)

    for i, distance in enumerate(distances):

        @pl.when(jnp.logical_not(there(-distance)))
        def _():
            for e in range(2):
                mix_in[e, i] = jnp.zeros(mix_in.shape[2:], f32)

    for o in range(offsets):
        for s in range(slots):
            at = jnp.minimum(send[0, o, s], own - 1)
            guess_out[o, s : s + 1, :] = guess[pl.ds(at, 1), :]
    for o in range(offsets):
        for s in range(slots):
            links[o * slots + s : o * slots + s + 1, :] = jnp.full(
                (1, LANES), send[0, o, s], jnp.int32
            )
    pl.semaphore_wait(
        barrier, jnp.minimum(me, reach) + jnp.minimum(n - 1 - me, reach)
    )
    for o in range(offsets):
        when_there(-shifts[o], lambda o=o: guess_copy(o).start())
    for o in range(offsets):
        when_there(-shifts[o], lambda o=o: link_copy(o).start())
    next_round(0)
    table[0, 0:own] = guess[...]

    def lay(r, carry):
        for j in range(LAY):
            at = pl.multiple_of((r * LAY + j) * LANES, LANES)
            for c in range(3):
                lane[pl.ds(c * rows + r * LAY + j, 1), :] = corners[c : c + 1, pl.ds(at, LANES)]
            for c in range(4):
                elem[pl.ds(c * rows + r * LAY + j, 1), :] = gradients[c : c + 1, pl.ds(at, LANES)]
        return carry

    lax.fori_loop(0, rows // LAY, lay, 0)

    wide = lax.broadcasted_iota(jnp.int32, (ROWS, LANES), 1)
    lookup = jnp.where(wide < own, wide, 2 * LANES)
    for o in range(offsets):
        for s in range(slots):
            lookup = jnp.where(wide == own + recv[0, o, s], own + o * slots + s, lookup)
    lookup = jnp.where(wide < nodes, lookup, 2 * LANES)

    for g in range(3 * groups):
        node = lane[g * ROWS : (g + 1) * ROWS, :]
        block = lax.shift_right_logical(node, 7)
        blk[g * ROWS : (g + 1) * ROWS, :] = jnp.take_along_axis(
            lookup, block, axis=1, mode="promise_in_bounds"
        )
        lane[g * ROWS : (g + 1) * ROWS, :] = lax.bitwise_and(node, LANES - 1)

    tall = lax.broadcasted_iota(jnp.int32, (LANES, LANES), 0)

    def heat(g, carry):
        at = pl.multiple_of(g * ROWS, ROWS)
        for j in range(ROWS):
            row = lane[pl.ds(at + j, 1), :]
            hot[pl.ds(pl.multiple_of((at + j) * LANES, LANES), LANES), :] = (
                jnp.where(row == tall, 1.0, 0.0).astype(bf16).T
            )
        return carry

    lax.fori_loop(0, 3 * groups, heat, 0)
    for o in range(offsets):
        when_there(shifts[o], lambda o=o: guess_copy(o).wait_recv())
    next_round(1)

    own_names = lax.broadcasted_iota(jnp.int32, (own, LANES), 0)
    all_names = lax.broadcasted_iota(jnp.int32, (nodes, LANES), 0)

    def at_corner(c, g):
        return pl.ds(pl.multiple_of(c * rows + g * ROWS, ROWS), ROWS)

    def operate(t):
        def picked(c, g, count):
            index = lane[at_corner(c, g), :]
            block = blk[at_corner(c, g), :]
            value = jnp.zeros((ROWS, LANES), f32)
            for b in range(count):
                row = jnp.broadcast_to(table[t, b : b + 1, :], (ROWS, LANES))
                got = jnp.take_along_axis(row, index, axis=1, mode="promise_in_bounds")
                value = jnp.where(block == b, got, value)
            return value

        def spread(g, energy):
            u = [picked(0, g, own), picked(1, g, nodes), picked(2, g, nodes)]
            if t > 0:
                for c in range(3):
                    vals[t - 1, at_corner(c, g), :] = u[c]
            adds, local_energy = element(g, u, t == 1)
            for c in range(3):
                top = adds[c].astype(bf16).astype(f32)
                hi[at_corner(c, g), :] = top
                lo[at_corner(c, g), :] = adds[c] - top
            return energy + local_energy if t == 1 else energy

        def summed(g, sums):
            first, rest = sums

            def product(c, names):
                parts = []
                at = pl.multiple_of(c * rows + g * ROWS, ROWS)
                for j in range(ROWS):
                    mask = blk[pl.ds(at + j, 1), :] == names
                    parts.append(
                        jnp.concatenate(
                            [
                                jnp.where(mask, hi[pl.ds(at + j, 1), :], 0.0),
                                jnp.where(mask, lo[pl.ds(at + j, 1), :], 0.0),
                            ],
                            axis=0,
                        ).astype(bf16)
                    )
                left = jnp.concatenate(parts, axis=1)
                right = hot[pl.ds(pl.multiple_of(at * LANES, ROWS * LANES), ROWS * LANES), :]
                return jnp.dot(left, right, preferred_element_type=f32)

            first = first + product(0, own_names)
            rest = rest + product(1, all_names) + product(2, all_names)
            return first, rest

        def step(g, carry):
            sums, energy = carry
            sums = summed(g, sums)
            energy = spread(g + 1, energy)
            return sums, energy

        sums = (jnp.zeros((2 * own, LANES), f32), jnp.zeros((2 * nodes, LANES), f32))
        energy = spread(0, jnp.zeros((ROWS, LANES), f32))
        sums, energy = lax.fori_loop(0, groups - 1, step, (sums, energy))
        first, rest = summed(groups - 1, sums)
        total = rest[:nodes] + rest[nodes:]
        return total[:own] + (first[:own] + first[own:]), total[own:], energy

    def element(g, u, with_energy):
        gx0, gy0, gx1, gy1 = [elem[at_corner(c, g), :] for c in range(4)]
        here = pl.ds(pl.multiple_of(g * ROWS, ROWS), ROWS)
        size = area[here, :]
        scaled = depth[here, :] * size
        third = size / 3.0
        from0, from1 = u[0] - u[2], u[1] - u[2]
        raw_x = gx0 * from0 + gx1 * from1
        raw_y = gy0 * from0 + gy1 * from1
        slope_x = scaled * raw_x
        slope_y = scaled * raw_y
        flow0 = gx0 * slope_x + gy0 * slope_y
        flow1 = gx1 * slope_x + gy1 * slope_y
        adds = [
            flow0 + third * u[0],
            flow1 + third * u[1],
            third * u[2] - (flow0 + flow1),
        ]
        if not with_energy:
            return adds, None
        return adds, (
            slope_x * raw_x
            + slope_y * raw_y
            + third * (u[0] * u[0] + u[1] * u[1] + u[2] * u[2])
        )

    def exchange(e, own_part, halo_part):
        base[...] = own_part
        for i, distance in enumerate(distances):
            for j, (mine, theirs) in enumerate(pairs[distance]):
                if mine == 0:
                    o = shifts.index(theirs)
                    for s in range(slots):
                        at = jnp.minimum(send[0, o, s], own - 1)
                        mix_out[e, i, j, s : s + 1, :] = base[pl.ds(at, 1), :]
                else:
                    o = shifts.index(mine)
                    mix_out[e, i, j] = halo_part[o * slots : (o + 1) * slots]
        for i, distance in enumerate(distances):
            when_there(distance, lambda i=i: mix_copy(e, i).start())

    def collect(e, own_part, halo_part):
        for i, distance in enumerate(distances):
            when_there(-distance, lambda i=i: mix_copy(e, i).wait_recv())
        own_total = own_part
        halo_total = [halo_part[o * slots : (o + 1) * slots] for o in range(offsets)]
        for i, distance in enumerate(distances):
            for j, (theirs, mine) in enumerate(pairs[distance]):
                if mine == 0:
                    own_total = owned(own_total, shifts.index(theirs), mix_in.at[e, i, j])
                elif theirs == 0:
                    o = shifts.index(mine)
                    halo_total[o] = halo_total[o] + mix_in[e, i, j]
                else:
                    o, p = shifts.index(mine), shifts.index(theirs)
                    names = links_in[o, o * slots : (o + 1) * slots]
                    for s in range(slots):
                        at = p * slots + s
                        halo_total[o] = halo_total[o] + jnp.where(
                            names == links_in[o, at : at + 1, :], mix_in[e, i, j, s : s + 1, :], 0.0
                        )
        return own_total, halo_total

    def owned(total, o, part):
        for s in range(slots):
            total = total + jnp.where(own_names == send[0, o, s], part[s : s + 1, :], 0.0)
        return total

    def fill(t, own_total, halo_total):
        table[t, 0:own] = own_total
        for o in range(offsets):
            table[t, own + o * slots : own + (o + 1) * slots] = halo_total[o]

    small = lax.broadcasted_iota(jnp.int32, (1, LANES), 1)

    def whole(a):
        return jnp.sum(jnp.sum(a, axis=0, keepdims=True), axis=1, keepdims=True)

    def start_sum(k, terms):
        line = jnp.zeros((1, LANES), f32)
        for i, term in enumerate(terms):
            line = jnp.where(small == i, whole(term), line)
        sum_out[k] = line
        sum_in[k, me] = line

        def push(i, carry):
            pltpu.make_async_remote_copy(
                src_ref=sum_out.at[k],
                dst_ref=sum_in.at[k, me],
                send_sem=sum_send_sem.at[k],
                recv_sem=sum_recv_sem.at[k],
                device_id=(lax.rem(me + 1 + lax.rem(i + n // 2, n - 1), n),),
                device_id_type=pl.DeviceIdType.MESH,
            ).start()
            return carry

        lax.fori_loop(0, n - 1, push, 0)

    def sum_bytes(k):
        return sum_in.at[k, pl.ds(0, n - 1)]

    def finish_sum(k, count):
        pltpu.make_async_copy(sum_bytes(k), sum_bytes(k), sum_recv_sem.at[k]).wait()
        line = jnp.sum(sum_in[k], axis=0)
        return [
            jnp.sum(jnp.where(small == i, line, 0.0), axis=1, keepdims=True)
            for i in range(count)
        ]

    own_part, halo_part, _ = operate(0)
    own_part, halo_part = forcing[...] - own_part, -halo_part
    exchange(0, own_part, halo_part)
    next_round(2)
    for o in range(offsets):
        when_there(shifts[o], lambda o=o: link_copy(o).wait_recv())
    own_total, halo_total = collect(0, own_part, halo_part)
    fill(1, own_total, halo_total)
    for i in range(3, len(rounds) + 1):
        next_round(i)

    own_part, halo_part, energy = operate(1)
    exchange(1, own_part, halo_part)
    residual = table[1, 0:own]
    start_sum(0, [residual * residual, energy])
    own_total, halo_total = collect(1, own_part, halo_part)
    fill(2, own_total, halo_total)

    own_part, halo_part, _ = operate(2)
    for o in range(offsets):
        back_out[o] = halo_part[o * slots : (o + 1) * slots]
    for o in range(offsets):
        when_there(shifts[o], lambda o=o: back_copy(o).start())

    norm, crossed = finish_sum(0, 2)
    step = norm / crossed

    def pair_energy(g, energy):
        u = [
            vals[0, at_corner(c, g), :] - step * vals[1, at_corner(c, g), :] for c in range(3)
        ]
        return energy + element(g, u, True)[1]

    energy = lax.fori_loop(0, groups, pair_energy, jnp.zeros((ROWS, LANES), f32))
    residual, image = table[1, 0:own], table[2, 0:own]
    later = residual - step * image
    start_sum(1, [later * later, energy, later * image])

    for o in range(offsets):
        when_there(-shifts[o], lambda o=o: back_copy(o).wait_recv())
    for o in range(offsets):
        own_part = owned(own_part, o, back_in.at[o])
    applied = image - step * own_part
    for o in range(offsets):
        when_there(-shifts[o], lambda o=o: guess_copy(o).wait_send())
        when_there(-shifts[o], lambda o=o: link_copy(o).wait_send())
        when_there(shifts[o], lambda o=o: back_copy(o).wait_send())
    for e in range(2):
        for i, distance in enumerate(distances):
            when_there(distance, lambda e=e, i=i: mix_copy(e, i).wait_send())
    fresh, own_pair, mixed = finish_sum(1, 3)
    beta = fresh / norm
    next_step = fresh / (own_pair + beta * (2.0 * mixed + beta * crossed))
    both[0:own] = guess[...] + step * residual + next_step * (later + beta * residual)
    both[own : 2 * own] = later - next_step * (applied + beta * image)
    for k in range(2):
        pltpu.make_async_copy(sum_bytes(k), sum_bytes(k), sum_send_sem.at[k]).wait()


def local(
    n,
    forcing,
    first_guess,
    corners,
    gradients,
    element_area,
    element_depth,
    send_blocks,
    recv_blocks,
):
    own, columns = forcing.shape
    _, offsets, slots = send_blocks.shape
    count = element_area.shape[0]
    rows = count // LANES
    nodes = own + offsets * slots
    assert columns == LANES and nodes <= LANES and rows % ROWS == 0 and slots % ROWS == 0
    f32 = jnp.float32
    vmem = pl.BlockSpec(memory_space=pltpu.VMEM)
    smem = pl.BlockSpec(memory_space=pltpu.SMEM)
    dma = pltpu.SemaphoreType.DMA
    pairs = message_pairs(shift_list(offsets))
    most = max(len(listed) for listed in pairs.values())
    part = (offsets, slots, LANES)
    mix = (2, len(pairs), most, slots, LANES)
    both = pl.pallas_call(
        functools.partial(kernel, n),
        out_shape=jax.ShapeDtypeStruct((2 * own, columns), f32),
        in_specs=[vmem] * 6 + [smem] * 2,
        out_specs=vmem,
        scratch_shapes=[
            pltpu.VMEM((3 * rows, LANES), jnp.int32),
            pltpu.VMEM((3 * rows, LANES), jnp.int32),
            pltpu.VMEM((3 * count, LANES), jnp.bfloat16),
            pltpu.VMEM((4 * rows, LANES), f32),
            pltpu.VMEM((2, 3 * rows, LANES), f32),
            pltpu.VMEM((3 * rows, LANES), f32),
            pltpu.VMEM((3 * rows, LANES), f32),
            pltpu.VMEM((3, nodes, LANES), f32),
            pltpu.VMEM((own, LANES), f32),
            pltpu.VMEM((offsets * slots, LANES), jnp.int32),
            pltpu.VMEM((offsets, offsets * slots, LANES), jnp.int32),
            pltpu.VMEM(part, f32),
            pltpu.VMEM(mix, f32),
            pltpu.VMEM(mix, f32),
            pltpu.VMEM(part, f32),
            pltpu.VMEM(part, f32),
            pltpu.VMEM((2, 1, LANES), f32),
            pltpu.VMEM((2, n, 1, LANES), f32),
            dma((offsets,)),
            dma((offsets,)),
            dma((offsets,)),
            dma((offsets,)),
            dma((2, len(pairs))),
            dma((2, len(pairs))),
            dma((offsets,)),
            dma((offsets,)),
            dma((2,)),
            dma((2,)),
            pltpu.SemaphoreType.REGULAR((len(learning_rounds(n, max(pairs))) + 1, 2)),
        ],
        compiler_params=pltpu.CompilerParams(collective_id=0, has_side_effects=True),
    )(
        forcing,
        first_guess,
        corners,
        gradients,
        element_area.reshape(rows, LANES),
        element_depth.reshape(rows, LANES),
        send_blocks,
        recv_blocks,
    )
    return both[:own], both[own:]


def solution(mesh):
    placed = (
        P("dom", None),
        P("dom", None),
        P(None, "dom"),
        P(None, "dom"),
        P("dom"),
        P("dom"),
        P("dom", None, None),
        P("dom", None, None),
    )
    return jax.shard_map(
        functools.partial(local, mesh.shape["dom"]),
        mesh=mesh,
        in_specs=placed,
        out_specs=(P("dom", None), P("dom", None)),
        check_vma=False,
    )
```

time: 38.5 us -> 34.9 us (0.906)
  Pallas kernels: 36.3 us -> 32.6 us
    pallas_call x1, Pallas kernels: 36.3 us -> 32.6 us  [local(): pl.pallas_call(functools.partial(kernel, n), out_shape=jax.ShapeDtypeStru...]
where the time goes in v1:
time: 34.9 us; the launch traced here: 34.6 us
  Pallas kernels  32.6 us (93%)
  local copies, waits for them, and re-layouts  1.35 us (4%)
  between operations  0.64 us (2%)
    pallas_call x1, Pallas kernels, local(): pl.pallas_call(functools.partial(kernel, n), out_shape=jax.ShapeDtypeStru...  32.6 us
    slice x1, local copies, waits for them, and re-layouts, local(): return (both[:own], both[own:])  1.35 us

profile of v1, /device:TPU:0, one launch (start us, length us, event | category | flops | bytes accessed | tf_op | source)
XLA Modules:
  0.0 34.6 jit_solution(4154978694396203762)
XLA Ops:
  0.6 32.6 %shard_map.95 = f32[64,128]{1,0:T(8,128)} custom-call(f32[32,128]{1,0:T(8,128)} %forcing.1, f32[32,128]{1,0:T(8,128)} %guess.1, s32[3,8192]{1,0:T(4,128)} %corners.1, f32[4,8192]{1,0:T(4,128)} %gradients.1, f32[64,128]{1,0:T(8,128)} %bitcast.2, f32[64,128]{1,0:T(8,128)} %bitcast.3, s32[1,4,8]{2,1,0:T(4,128)} %send.1, s32[1,4,8]{2,1,0:T(4,128)} %recv.1), custom_call_target="tpu_custom_call" | custom-call | tf_op jit(solution)/shard_map/pallas_call | solution.py:522
  33.3 1.3 %fusion = (f32[32,128]{1,0:T(8,128)}, f32[32,128]{1,0:T(8,128)}) fusion(f32[64,128]{1,0:T(8,128)} %shard_map.95), kind=kLoop, calls=%fused_computation | loop fusion | bytes 65536 | tf_op jit(solution)/shard_map/slice | solution.py:569

commit v2 on v1

--- a/solution.py
+++ b/solution.py
@@ -9,7 +9,8 @@
 
 LANES = 128
 ROWS = 8
-LAY = 8
+HEAT = 6
+STEP = 2
 
 
 def shift_list(offsets):
@@ -50,6 +51,7 @@
     recv,
     both,
     blk,
+    name,
     lane,
     hot,
     elem,
@@ -83,6 +85,7 @@
     _, offsets, slots = send.shape
     halo = offsets * slots
     nodes = own + halo
+    wide_rows = max(own, halo)
     rows = area.shape[0]
     groups = rows // ROWS
     shifts = shift_list(offsets)
@@ -218,15 +221,15 @@
     table[0, 0:own] = guess[...]
 
     def lay(r, carry):
-        for j in range(LAY):
-            at = pl.multiple_of((r * LAY + j) * LANES, LANES)
+        for j in range(ROWS):
+            at = pl.multiple_of((r * ROWS + j) * LANES, LANES)
             for c in range(3):
-                lane[pl.ds(c * rows + r * LAY + j, 1), :] = corners[c : c + 1, pl.ds(at, LANES)]
+                lane[pl.ds((r * 3 + c) * ROWS + j, 1), :] = corners[c : c + 1, pl.ds(at, LANES)]
             for c in range(4):
-                elem[pl.ds(c * rows + r * LAY + j, 1), :] = gradients[c : c + 1, pl.ds(at, LANES)]
+                elem[pl.ds((r * 4 + c) * ROWS + j, 1), :] = gradients[c : c + 1, pl.ds(at, LANES)]
         return carry
 
-    lax.fori_loop(0, rows // LAY, lay, 0)
+    lax.fori_loop(0, groups, lay, 0)
 
     wide = lax.broadcasted_iota(jnp.int32, (ROWS, LANES), 1)
     lookup = jnp.where(wide < own, wide, 2 * LANES)
@@ -236,34 +239,38 @@
     lookup = jnp.where(wide < nodes, lookup, 2 * LANES)
 
     for g in range(3 * groups):
-        node = lane[g * ROWS : (g + 1) * ROWS, :]
-        block = lax.shift_right_logical(node, 7)
-        blk[g * ROWS : (g + 1) * ROWS, :] = jnp.take_along_axis(
-            lookup, block, axis=1, mode="promise_in_bounds"
-        )
-        lane[g * ROWS : (g + 1) * ROWS, :] = lax.bitwise_and(node, LANES - 1)
+        here = slice(g * ROWS, (g + 1) * ROWS)
+        node = lane[here, :]
+        block = jnp.take_along_axis(
+            lookup, lax.shift_right_logical(node, 7), axis=1, mode="promise_in_bounds"
+        )
+        blk[here, :] = block
+        name[here, :] = jnp.where(block < own, block, block - own)
+        hi[here, :] = jnp.where(block < own, 1.0, -1.0)
+        lane[here, :] = lax.bitwise_and(node, LANES - 1)
 
     tall = lax.broadcasted_iota(jnp.int32, (LANES, LANES), 0)
 
     def heat(g, carry):
-        at = pl.multiple_of(g * ROWS, ROWS)
-        for j in range(ROWS):
-            row = lane[pl.ds(at + j, 1), :]
-            hot[pl.ds(pl.multiple_of((at + j) * LANES, LANES), LANES), :] = (
-                jnp.where(row == tall, 1.0, 0.0).astype(bf16).T
-            )
+        for j in range(HEAT * ROWS):
+            at = g * (HEAT * ROWS) + j
+            code = jnp.where(lane[pl.ds(at, 1), :] == tall, hi[pl.ds(at, 1), :], 0.0)
+            code = code.astype(bf16).T
+            to = pl.ds(pl.multiple_of(at * LANES, LANES), LANES)
+            hot[to, 0:LANES] = jnp.maximum(code, 0.0).astype(hot.dtype)
+            hot[to, LANES : 2 * LANES] = jnp.maximum(-code, 0.0).astype(hot.dtype)
         return carry
 
-    lax.fori_loop(0, 3 * groups, heat, 0)
+    lax.fori_loop(0, 3 * groups // HEAT, heat, 0)
     for o in range(offsets):
         when_there(shifts[o], lambda o=o: guess_copy(o).wait_recv())
     next_round(1)
 
     own_names = lax.broadcasted_iota(jnp.int32, (own, LANES), 0)
-    all_names = lax.broadcasted_iota(jnp.int32, (nodes, LANES), 0)
+    names = lax.broadcasted_iota(jnp.int32, (wide_rows, LANES), 0)
 
     def at_corner(c, g):
-        return pl.ds(pl.multiple_of(c * rows + g * ROWS, ROWS), ROWS)
+        return pl.ds(pl.multiple_of((g * 3 + c) * ROWS, ROWS), ROWS)
 
     def operate(t):
         def picked(c, g, count):
@@ -289,45 +296,49 @@
             return energy + local_energy if t == 1 else energy
 
         def summed(g, sums):
-            first, rest = sums
-
-            def product(c, names):
-                parts = []
-                at = pl.multiple_of(c * rows + g * ROWS, ROWS)
-                for j in range(ROWS):
-                    mask = blk[pl.ds(at + j, 1), :] == names
-                    parts.append(
-                        jnp.concatenate(
-                            [
-                                jnp.where(mask, hi[pl.ds(at + j, 1), :], 0.0),
-                                jnp.where(mask, lo[pl.ds(at + j, 1), :], 0.0),
-                            ],
-                            axis=0,
-                        ).astype(bf16)
-                    )
-                left = jnp.concatenate(parts, axis=1)
-                right = hot[pl.ds(pl.multiple_of(at * LANES, ROWS * LANES), ROWS * LANES), :]
-                return jnp.dot(left, right, preferred_element_type=f32)
-
-            first = first + product(0, own_names)
-            rest = rest + product(1, all_names) + product(2, all_names)
-            return first, rest
-
-        def step(g, carry):
+            first = pl.multiple_of(g * (3 * ROWS), 3 * ROWS)
+            parts = []
+            for j in range(STEP * 3 * ROWS):
+                mask = name[pl.ds(first + j, 1), :] == names
+                parts.append(
+                    jnp.concatenate(
+                        [
+                            jnp.where(mask, hi[pl.ds(first + j, 1), :], 0.0),
+                            jnp.where(mask, lo[pl.ds(first + j, 1), :], 0.0),
+                        ],
+                        axis=0,
+                    ).astype(bf16)
+                )
+            count = STEP * 3 * ROWS * LANES
+            return sums + lax.dot_general(
+                jnp.concatenate(parts, axis=1),
+                hot[pl.ds(pl.multiple_of(first * LANES, 3 * ROWS * LANES), count), :],
+                (((1,), (0,)), ((), ())),
+                preferred_element_type=f32,
+            )
+
+        def spread_some(g, energy):
+            for k in range(STEP):
+                energy = spread(g + k, energy)
+            return energy
+
+        def step(i, carry):
             sums, energy = carry
-            sums = summed(g, sums)
-            energy = spread(g + 1, energy)
+            sums = summed(i * STEP, sums)
+            energy = spread_some((i + 1) * STEP, energy)
             return sums, energy
 
-        sums = (jnp.zeros((2 * own, LANES), f32), jnp.zeros((2 * nodes, LANES), f32))
-        energy = spread(0, jnp.zeros((ROWS, LANES), f32))
-        sums, energy = lax.fori_loop(0, groups - 1, step, (sums, energy))
-        first, rest = summed(groups - 1, sums)
-        total = rest[:nodes] + rest[nodes:]
-        return total[:own] + (first[:own] + first[own:]), total[own:], energy
+        sums = jnp.zeros((2 * wide_rows, 2 * LANES), f32)
+        energy = spread_some(0, jnp.zeros((ROWS, LANES), f32))
+        sums, energy = lax.fori_loop(0, groups // STEP - 1, step, (sums, energy))
+        sums = summed(groups - STEP, sums)
+        sums = sums[:wide_rows] + sums[wide_rows:]
+        return sums[:own, :LANES], sums[:halo, LANES:], energy
 
     def element(g, u, with_energy):
-        gx0, gy0, gx1, gy1 = [elem[at_corner(c, g), :] for c in range(4)]
+        gx0, gy0, gx1, gy1 = [
+            elem[pl.ds(pl.multiple_of((g * 4 + c) * ROWS, ROWS), ROWS), :] for c in range(4)
+        ]
         here = pl.ds(pl.multiple_of(g * ROWS, ROWS), ROWS)
         size = area[here, :]
         scaled = depth[here, :] * size
@@ -510,7 +521,8 @@
     count = element_area.shape[0]
     rows = count // LANES
     nodes = own + offsets * slots
-    assert columns == LANES and nodes <= LANES and rows % ROWS == 0 and slots % ROWS == 0
+    assert columns == LANES and nodes <= LANES and slots % ROWS == 0
+    assert rows % (ROWS * STEP) == 0 and (3 * rows // ROWS) % HEAT == 0
     f32 = jnp.float32
     vmem = pl.BlockSpec(memory_space=pltpu.VMEM)
     smem = pl.BlockSpec(memory_space=pltpu.SMEM)
@@ -527,7 +539,8 @@
         scratch_shapes=[
             pltpu.VMEM((3 * rows, LANES), jnp.int32),
             pltpu.VMEM((3 * rows, LANES), jnp.int32),
-            pltpu.VMEM((3 * count, LANES), jnp.bfloat16),
+            pltpu.VMEM((3 * rows, LANES), jnp.int32),
+            pltpu.VMEM((3 * count, 2 * LANES), jnp.float8_e4m3fn),
             pltpu.VMEM((4 * rows, LANES), f32),
             pltpu.VMEM((2, 3 * rows, LANES), f32),
             pltpu.VMEM((3 * rows, LANES), f32),

time: 34.9 us -> 32.4 us (0.928)
  Pallas kernels: 32.6 us -> 30.2 us
    pallas_call x1, Pallas kernels: 32.6 us -> 30.2 us  [local(): pl.pallas_call(functools.partial(kernel, n), out_shape=jax.ShapeDtypeStru...]
where the time goes in v2:
time: 32.4 us; the launch traced here: 32.2 us
  Pallas kernels  30.2 us (93%)
  local copies, waits for them, and re-layouts  1.35 us (4%)
  between operations  0.64 us (2%)
    pallas_call x1, Pallas kernels, local(): pl.pallas_call(functools.partial(kernel, n), out_shape=jax.ShapeDtypeStru...  30.2 us
    slice x1, local copies, waits for them, and re-layouts, local(): return (both[:own], both[own:])  1.35 us

profile of v2, /device:TPU:0, one launch (start us, length us, event | category | flops | bytes accessed | tf_op | source)
XLA Modules:
  0.0 32.2 jit_solution(2275331237488566453)
XLA Ops:
  0.6 30.2 %shard_map.95 = f32[64,128]{1,0:T(8,128)} custom-call(f32[32,128]{1,0:T(8,128)} %forcing.1, f32[32,128]{1,0:T(8,128)} %guess.1, s32[3,8192]{1,0:T(4,128)} %corners.1, f32[4,8192]{1,0:T(4,128)} %gradients.1, f32[64,128]{1,0:T(8,128)} %bitcast.2, f32[64,128]{1,0:T(8,128)} %bitcast.3, s32[1,4,8]{2,1,0:T(4,128)} %send.1, s32[1,4,8]{2,1,0:T(4,128)} %recv.1), custom_call_target="tpu_custom_call" | custom-call | tf_op jit(solution)/shard_map/pallas_call | solution.py:534
  30.8 1.3 %fusion = (f32[32,128]{1,0:T(8,128)}, f32[32,128]{1,0:T(8,128)}) fusion(f32[64,128]{1,0:T(8,128)} %shard_map.95), kind=kLoop, calls=%fused_computation | loop fusion | bytes 65536 | tf_op jit(solution)/shard_map/slice | solution.py:582

commit v3 on v2

--- a/solution.py
+++ b/solution.py
@@ -11,6 +11,7 @@
 ROWS = 8
 HEAT = 6
 STEP = 2
+PUSH = 8
 
 
 def shift_list(offsets):
@@ -41,6 +42,15 @@
 
 def kernel(
     n,
+    forcing_in,
+    guess_in,
+    corners_in,
+    gradients_in,
+    area_in,
+    depth_in,
+    send_in,
+    recv_in,
+    both,
     forcing,
     guess,
     corners,
@@ -49,7 +59,7 @@
     depth,
     send,
     recv,
-    both,
+    load_sem,
     blk,
     name,
     lane,
@@ -92,6 +102,7 @@
     pairs = message_pairs(shifts)
     distances = list(pairs)
     reach = max(distances)
+    order = sorted(distances, key=lambda distance: (-abs(distance), distance))
     me = lax.axis_index("dom")
     f32 = jnp.float32
     bf16 = jnp.bfloat16
@@ -143,6 +154,23 @@
             back_out.at[o], back_in.at[o], back_send_sem.at[o], back_recv_sem.at[o], shifts[o]
         )
 
+    loads = [
+        pltpu.make_async_copy(source, target, load_sem.at[i])
+        for i, (source, target) in enumerate(
+            [
+                (send_in, send),
+                (guess_in, guess),
+                (corners_in, corners),
+                (recv_in, recv),
+                (gradients_in, gradients),
+                (area_in, area),
+                (depth_in, depth),
+                (forcing_in, forcing),
+            ]
+        )
+    ]
+    for load in loads[:3]:
+        load.start()
     barrier = pltpu.get_barrier_semaphore()
     for distance in distances:
         when_there(
@@ -155,6 +183,8 @@
             ),
         )
 
+    for load in loads[3:]:
+        load.start()
     rounds = learning_rounds(n, reach)
 
     def tell(i):
@@ -183,24 +213,8 @@
         if i < len(rounds):
             tell(i)
 
-    for o in range(offsets):
-
-        @pl.when(jnp.logical_not(there(shifts[o])))
-        def _():
-            table[0, own + o * slots : own + (o + 1) * slots] = jnp.zeros((slots, LANES), f32)
-            links_in[o] = jnp.full((halo, LANES), own, jnp.int32)
-
-        @pl.when(jnp.logical_not(there(-shifts[o])))
-        def _():
-            back_in[o] = jnp.zeros((slots, LANES), f32)
-
-    for i, distance in enumerate(distances):
-
-        @pl.when(jnp.logical_not(there(-distance)))
-        def _():
-            for e in range(2):
-                mix_in[e, i] = jnp.zeros(mix_in.shape[2:], f32)
-
+    for load in loads[:2]:
+        load.wait()
     for o in range(offsets):
         for s in range(slots):
             at = jnp.minimum(send[0, o, s], own - 1)
@@ -218,7 +232,26 @@
     for o in range(offsets):
         when_there(-shifts[o], lambda o=o: link_copy(o).start())
     next_round(0)
+    for o in range(offsets):
+
+        @pl.when(jnp.logical_not(there(shifts[o])))
+        def _():
+            table[0, own + o * slots : own + (o + 1) * slots] = jnp.zeros((slots, LANES), f32)
+            links_in[o] = jnp.full((halo, LANES), own, jnp.int32)
+
+        @pl.when(jnp.logical_not(there(-shifts[o])))
+        def _():
+            back_in[o] = jnp.zeros((slots, LANES), f32)
+
+    for i, distance in enumerate(distances):
+
+        @pl.when(jnp.logical_not(there(-distance)))
+        def _():
+            for e in range(2):
+                mix_in[e, i] = jnp.zeros(mix_in.shape[2:], f32)
     table[0, 0:own] = guess[...]
+    for load in loads[2:5]:
+        load.wait()
 
     def lay(r, carry):
         for j in range(ROWS):
@@ -262,6 +295,8 @@
         return carry
 
     lax.fori_loop(0, 3 * groups // HEAT, heat, 0)
+    for load in loads[5:]:
+        load.wait()
     for o in range(offsets):
         when_there(shifts[o], lambda o=o: guess_copy(o).wait_recv())
     next_round(1)
@@ -272,7 +307,7 @@
     def at_corner(c, g):
         return pl.ds(pl.multiple_of((g * 3 + c) * ROWS, ROWS), ROWS)
 
-    def operate(t):
+    def operate(t, gathered=None):
         def picked(c, g, count):
             index = lane[at_corner(c, g), :]
             block = blk[at_corner(c, g), :]
@@ -331,6 +366,8 @@
         sums = jnp.zeros((2 * wide_rows, 2 * LANES), f32)
         energy = spread_some(0, jnp.zeros((ROWS, LANES), f32))
         sums, energy = lax.fori_loop(0, groups // STEP - 1, step, (sums, energy))
+        if gathered is not None:
+            gathered()
         sums = summed(groups - STEP, sums)
         sums = sums[:wide_rows] + sums[wide_rows:]
         return sums[:own, :LANES], sums[:halo, LANES:], energy
@@ -365,7 +402,8 @@
 
     def exchange(e, own_part, halo_part):
         base[...] = own_part
-        for i, distance in enumerate(distances):
+        for distance in reversed(order):
+            i = distances.index(distance)
             for j, (mine, theirs) in enumerate(pairs[distance]):
                 if mine == 0:
                     o = shifts.index(theirs)
@@ -375,15 +413,14 @@
                 else:
                     o = shifts.index(mine)
                     mix_out[e, i, j] = halo_part[o * slots : (o + 1) * slots]
-        for i, distance in enumerate(distances):
             when_there(distance, lambda i=i: mix_copy(e, i).start())
 
     def collect(e, own_part, halo_part):
-        for i, distance in enumerate(distances):
-            when_there(-distance, lambda i=i: mix_copy(e, i).wait_recv())
         own_total = own_part
         halo_total = [halo_part[o * slots : (o + 1) * slots] for o in range(offsets)]
-        for i, distance in enumerate(distances):
+        for distance in order:
+            i = distances.index(distance)
+            when_there(-distance, lambda i=i: mix_copy(e, i).wait_recv())
             for j, (theirs, mine) in enumerate(pairs[distance]):
                 if mine == 0:
                     own_total = owned(own_total, shifts.index(theirs), mix_in.at[e, i, j])
@@ -422,18 +459,31 @@
         sum_out[k] = line
         sum_in[k, me] = line
 
-        def push(i, carry):
+        def push(ahead):
+            other = me + ahead
             pltpu.make_async_remote_copy(
                 src_ref=sum_out.at[k],
                 dst_ref=sum_in.at[k, me],
                 send_sem=sum_send_sem.at[k],
                 recv_sem=sum_recv_sem.at[k],
-                device_id=(lax.rem(me + 1 + lax.rem(i + n // 2, n - 1), n),),
+                device_id=(jnp.where(other >= n, other - n, other),),
                 device_id_type=pl.DeviceIdType.MESH,
             ).start()
-            return carry
-
-        lax.fori_loop(0, n - 1, push, 0)
+
+        def push_some(first, last):
+            steps = (last - first) // PUSH
+
+            def body(i, carry):
+                for j in range(PUSH):
+                    push(first + i * PUSH + j)
+                return carry
+
+            lax.fori_loop(0, steps, body, 0)
+            for ahead in range(first + steps * PUSH, last):
+                push(ahead)
+
+        push_some(n // 2, n)
+        push_some(1, n // 2)
 
     def sum_bytes(k):
         return sum_in.at[k, pl.ds(0, n - 1)]
@@ -464,25 +514,34 @@
     own_total, halo_total = collect(1, own_part, halo_part)
     fill(2, own_total, halo_total)
 
-    own_part, halo_part, _ = operate(2)
+    residual, image = table[1, 0:own], table[2, 0:own]
+    scalars = []
+
+    def second_sums():
+        norm, crossed = finish_sum(0, 2)
+        step = norm / crossed
+        scalars.extend([norm, crossed, step])
+
+        def pair_energy(g, energy):
+            u = [
+                vals[0, at_corner(c, g), :] - step * vals[1, at_corner(c, g), :]
+                for c in range(3)
+            ]
+            return energy + element(g, u, True)[1]
+
+        energy = jnp.zeros((ROWS, LANES), f32)
+        for g in range(groups):
+            energy = pair_energy(g, energy)
+        later = residual - step * image
+        start_sum(1, [later * later, energy, later * image])
+
+    own_part, halo_part, _ = operate(2, second_sums)
     for o in range(offsets):
         back_out[o] = halo_part[o * slots : (o + 1) * slots]
     for o in range(offsets):
         when_there(shifts[o], lambda o=o: back_copy(o).start())
-
-    norm, crossed = finish_sum(0, 2)
-    step = norm / crossed
-
-    def pair_energy(g, energy):
-        u = [
-            vals[0, at_corner(c, g), :] - step * vals[1, at_corner(c, g), :] for c in range(3)
-        ]
-        return energy + element(g, u, True)[1]
-
-    energy = lax.fori_loop(0, groups, pair_energy, jnp.zeros((ROWS, LANES), f32))
-    residual, image = table[1, 0:own], table[2, 0:own]
+    norm, crossed, step = scalars
     later = residual - step * image
-    start_sum(1, [later * later, energy, later * image])
 
     for o in range(offsets):
         when_there(-shifts[o], lambda o=o: back_copy(o).wait_recv())
@@ -525,7 +584,6 @@
     assert rows % (ROWS * STEP) == 0 and (3 * rows // ROWS) % HEAT == 0
     f32 = jnp.float32
     vmem = pl.BlockSpec(memory_space=pltpu.VMEM)
-    smem = pl.BlockSpec(memory_space=pltpu.SMEM)
     dma = pltpu.SemaphoreType.DMA
     pairs = message_pairs(shift_list(offsets))
     most = max(len(listed) for listed in pairs.values())
@@ -533,10 +591,19 @@
     mix = (2, len(pairs), most, slots, LANES)
     both = pl.pallas_call(
         functools.partial(kernel, n),
-        out_shape=jax.ShapeDtypeStruct((2 * own, columns), f32),
-        in_specs=[vmem] * 6 + [smem] * 2,
+        out_shape=pltpu.VMEM((2 * own, columns), f32),
+        in_specs=[pl.BlockSpec(memory_space=pl.ANY)] * 8,
         out_specs=vmem,
         scratch_shapes=[
+            pltpu.VMEM(forcing.shape, f32),
+            pltpu.VMEM(first_guess.shape, f32),
+            pltpu.VMEM(corners.shape, jnp.int32),
+            pltpu.VMEM(gradients.shape, f32),
+            pltpu.VMEM((rows, LANES), f32),
+            pltpu.VMEM((rows, LANES), f32),
+            pltpu.SMEM(send_blocks.shape, jnp.int32),
+            pltpu.SMEM(recv_blocks.shape, jnp.int32),
+            dma((8,)),
             pltpu.VMEM((3 * rows, LANES), jnp.int32),
             pltpu.VMEM((3 * rows, LANES), jnp.int32),
             pltpu.VMEM((3 * rows, LANES), jnp.int32),
@@ -568,7 +635,9 @@
             dma((2,)),
             pltpu.SemaphoreType.REGULAR((len(learning_rounds(n, max(pairs))) + 1, 2)),
         ],
-        compiler_params=pltpu.CompilerParams(collective_id=0, has_side_effects=True),
+        compiler_params=pltpu.CompilerParams(
+            collective_id=0, has_side_effects=True
+        ),
     )(
         forcing,
         first_guess,

time: 32.4 us -> 29.4 us (0.907)
  Pallas kernels: 30.2 us -> 27.9 us
  local copies, waits for them, and re-layouts: 1.35 us -> 0.61 us
    pallas_call x1, Pallas kernels: 30.2 us -> 27.9 us  [local(): pl.pallas_call(functools.partial(kernel, n), out_shape=pltpu.VMEM((2 * ow...]
    slice x1, local copies, waits for them, and re-layouts: 1.35 us -> 0.61 us  [local(): return (both[:own], both[own:])]
where the time goes in v3:
time: 29.4 us; the launch traced here: 29.2 us
  Pallas kernels  27.9 us (95%)
  between operations  0.64 us (2%)
  local copies, waits for them, and re-layouts  0.61 us (2%)
    pallas_call x1, Pallas kernels, local(): pl.pallas_call(functools.partial(kernel, n), out_shape=pltpu.VMEM((2 * ow...  27.9 us
    slice x1, local copies, waits for them, and re-layouts, local(): return (both[:own], both[own:])  0.61 us

profile of v3, /device:TPU:0, one launch (start us, length us, event | category | flops | bytes accessed | tf_op | source)
XLA Modules:
  0.0 29.2 jit_solution(6660285424208623148)
XLA Ops:
  0.6 27.9 %shard_map.95 = f32[64,128]{1,0:T(8,128)S(1)} custom-call(f32[32,128]{1,0:T(8,128)} %forcing_in.1, f32[32,128]{1,0:T(8,128)} %guess_in.1, s32[3,8192]{1,0:T(4,128)} %corners_in.1, f32[4,8192]{1,0:T(4,128)} %gradients_in.1, f32[64,128]{1,0:T(8,128)} %bitcast.2, f32[64,128]{1,0:T(8,128)} %bitcast.3, s32[1,4,8]{2,1,0:T(4,128)} %send_in.1, s32[1,4,8]{2,1,0:T(4,128)} %recv_in.1), custom_call_target="tpu_custom_call" | custom-call | tf_op jit(solution)/shard_map/pallas_call | solution.py:592
  28.6 0.6 %fusion = (f32[32,128]{1,0:T(8,128)}, f32[32,128]{1,0:T(8,128)}) fusion(f32[64,128]{1,0:T(8,128)S(1)} %shard_map.95), kind=kLoop, calls=%fused_computation | loop fusion | bytes 65536 | tf_op jit(solution)/shard_map/slice | solution.py:651

commit v4 on v3

--- a/solution.py
+++ b/solution.py
@@ -10,7 +10,7 @@
 LANES = 128
 ROWS = 8
 HEAT = 6
-STEP = 2
+PARTS = 2
 PUSH = 8
 
 
@@ -64,6 +64,8 @@
     name,
     lane,
     hot,
+    wide_hot,
+    split,
     elem,
     vals,
     hi,
@@ -288,7 +290,14 @@
         for j in range(HEAT * ROWS):
             at = g * (HEAT * ROWS) + j
             code = jnp.where(lane[pl.ds(at, 1), :] == tall, hi[pl.ds(at, 1), :], 0.0)
-            code = code.astype(bf16).T
+            code = code.astype(bf16)
+            block, row = divmod(j, ROWS)
+            if block % 3 == 1:
+                column = (g * (HEAT // 3) + block // 3) * ROWS + row
+                columns = pl.ds(pl.multiple_of(column * LANES, LANES), LANES)
+                wide_hot[0:LANES, columns] = jnp.maximum(code, 0.0).astype(hot.dtype)
+                wide_hot[LANES : 2 * LANES, columns] = jnp.maximum(-code, 0.0).astype(hot.dtype)
+            code = code.T
             to = pl.ds(pl.multiple_of(at * LANES, LANES), LANES)
             hot[to, 0:LANES] = jnp.maximum(code, 0.0).astype(hot.dtype)
             hot[to, LANES : 2 * LANES] = jnp.maximum(-code, 0.0).astype(hot.dtype)
@@ -306,6 +315,9 @@
 
     def at_corner(c, g):
         return pl.ds(pl.multiple_of((g * 3 + c) * ROWS, ROWS), ROWS)
+
+    sublane = lax.broadcasted_iota(jnp.int32, (ROWS, LANES), 0)
+    once = 1 + jnp.minimum(me, 0)
 
     def operate(t, gathered=None):
         def picked(c, g, count):
@@ -318,8 +330,37 @@
                 value = jnp.where(block == b, got, value)
             return value
 
+        def multiplied(g):
+            columns = pl.ds(pl.multiple_of(g * (ROWS * LANES), ROWS * LANES), ROWS * LANES)
+            product = lax.dot_general(
+                split[...],
+                wide_hot[:, columns],
+                (((1,), (0,)), ((), ())),
+                preferred_element_type=f32,
+            )
+            product = product[:wide_rows] + product[wide_rows:]
+            at = pl.multiple_of((g * 3 + 1) * ROWS, ROWS)
+            rows_left = []
+            for j in range(ROWS):
+                kept = jnp.where(
+                    name[pl.ds(at + j, 1), :] == names, product[:, j * LANES : (j + 1) * LANES], 0.0
+                )
+                kept = [kept[r : r + ROWS] for r in range(0, wide_rows, ROWS)]
+                while len(kept) > 1:
+                    kept = [a + b for a, b in zip(kept[::2], kept[1::2])]
+                rows_left.append(kept[0])
+            bit = 1
+            while bit < ROWS:
+                upper = jnp.bitwise_and(sublane, bit) != 0
+                rows_left = [
+                    jnp.where(upper, b, a) + pltpu.roll(jnp.where(upper, a, b), bit, axis=0)
+                    for a, b in zip(rows_left[::2], rows_left[1::2])
+                ]
+                bit *= 2
+            return rows_left[0]
+
         def spread(g, energy):
-            u = [picked(0, g, own), picked(1, g, nodes), picked(2, g, nodes)]
+            u = [picked(0, g, own), multiplied(g), picked(2, g, nodes)]
             if t > 0:
                 for c in range(3):
                     vals[t - 1, at_corner(c, g), :] = u[c]
@@ -330,45 +371,45 @@
                 lo[at_corner(c, g), :] = adds[c] - top
             return energy + local_energy if t == 1 else energy
 
-        def summed(g, sums):
-            first = pl.multiple_of(g * (3 * ROWS), 3 * ROWS)
+        def summed(first, last, sums):
             parts = []
-            for j in range(STEP * 3 * ROWS):
-                mask = name[pl.ds(first + j, 1), :] == names
+            for at in range(first * 3 * ROWS, last * 3 * ROWS):
+                mask = name[at : at + 1, :] == names
                 parts.append(
                     jnp.concatenate(
                         [
-                            jnp.where(mask, hi[pl.ds(first + j, 1), :], 0.0),
-                            jnp.where(mask, lo[pl.ds(first + j, 1), :], 0.0),
+                            jnp.where(mask, hi[at : at + 1, :], 0.0),
+                            jnp.where(mask, lo[at : at + 1, :], 0.0),
                         ],
                         axis=0,
                     ).astype(bf16)
                 )
-            count = STEP * 3 * ROWS * LANES
-            return sums + lax.dot_general(
+            product = lax.dot_general(
                 jnp.concatenate(parts, axis=1),
-                hot[pl.ds(pl.multiple_of(first * LANES, 3 * ROWS * LANES), count), :],
+                hot[first * 3 * ROWS * LANES : last * 3 * ROWS * LANES, :],
                 (((1,), (0,)), ((), ())),
                 preferred_element_type=f32,
             )
-
-        def spread_some(g, energy):
-            for k in range(STEP):
-                energy = spread(g + k, energy)
-            return energy
-
-        def step(i, carry):
-            sums, energy = carry
-            sums = summed(i * STEP, sums)
-            energy = spread_some((i + 1) * STEP, energy)
-            return sums, energy
-
+            return product if sums is None else sums + product
+
+        bounds = [-(-groups * i // PARTS) for i in range(PARTS + 1)]
+        energy = jnp.zeros((ROWS, LANES), f32)
+        for g in range(bounds[0], bounds[1]):
+            energy = spread(g, energy)
         sums = jnp.zeros((2 * wide_rows, 2 * LANES), f32)
-        energy = spread_some(0, jnp.zeros((ROWS, LANES), f32))
-        sums, energy = lax.fori_loop(0, groups // STEP - 1, step, (sums, energy))
+        for part in range(1, PARTS):
+
+            def step(_, carry, part=part):
+                sums, energy = carry
+                sums = summed(bounds[part - 1], bounds[part], sums)
+                for g in range(bounds[part], bounds[part + 1]):
+                    energy = spread(g, energy)
+                return sums, energy
+
+            sums, energy = lax.fori_loop(0, once, step, (sums, energy))
         if gathered is not None:
             gathered()
-        sums = summed(groups - STEP, sums)
+        sums = summed(bounds[PARTS - 1], groups, sums)
         sums = sums[:wide_rows] + sums[wide_rows:]
         return sums[:own, :LANES], sums[:halo, LANES:], energy
 
@@ -442,10 +483,18 @@
             total = total + jnp.where(own_names == send[0, o, s], part[s : s + 1, :], 0.0)
         return total
 
+    def divide(own_total, halo_total):
+        for side, total in enumerate([own_total, halo_total]):
+            columns = slice(side * LANES, (side + 1) * LANES)
+            top = total.astype(bf16)
+            split[0:own, columns] = top
+            split[own : 2 * own, columns] = (total - top.astype(f32)).astype(bf16)
+
     def fill(t, own_total, halo_total):
+        halo_total = jnp.concatenate(halo_total, axis=0)
         table[t, 0:own] = own_total
-        for o in range(offsets):
-            table[t, own + o * slots : own + (o + 1) * slots] = halo_total[o]
+        table[t, own:nodes] = halo_total
+        divide(own_total, halo_total)
 
     small = lax.broadcasted_iota(jnp.int32, (1, LANES), 1)
 
@@ -496,6 +545,7 @@
             for i in range(count)
         ]
 
+    divide(table[0, 0:own], table[0, own:nodes])
     own_part, halo_part, _ = operate(0)
     own_part, halo_part = forcing[...] - own_part, -halo_part
     exchange(0, own_part, halo_part)
@@ -581,7 +631,8 @@
     rows = count // LANES
     nodes = own + offsets * slots
     assert columns == LANES and nodes <= LANES and slots % ROWS == 0
-    assert rows % (ROWS * STEP) == 0 and (3 * rows // ROWS) % HEAT == 0
+    assert rows % ROWS == 0 and (3 * rows // ROWS) % HEAT == 0 and HEAT % 3 == 0
+    assert own == offsets * slots and own % (2 * ROWS) == 0
     f32 = jnp.float32
     vmem = pl.BlockSpec(memory_space=pltpu.VMEM)
     dma = pltpu.SemaphoreType.DMA
@@ -608,6 +659,8 @@
             pltpu.VMEM((3 * rows, LANES), jnp.int32),
             pltpu.VMEM((3 * rows, LANES), jnp.int32),
             pltpu.VMEM((3 * count, 2 * LANES), jnp.float8_e4m3fn),
+            pltpu.VMEM((2 * LANES, count), jnp.float8_e4m3fn),
+            pltpu.VMEM((2 * own, 2 * LANES), jnp.bfloat16),
             pltpu.VMEM((4 * rows, LANES), f32),
             pltpu.VMEM((2, 3 * rows, LANES), f32),
             pltpu.VMEM((3 * rows, LANES), f32),

time: 29.4 us -> 28.3 us (0.963)
  Pallas kernels: 27.9 us -> 26.9 us
    pallas_call x1, Pallas kernels: 27.9 us -> 26.9 us  [local(): pl.pallas_call(functools.partial(kernel, n), out_shape=pltpu.VMEM((2 * ow...]
where the time goes in v4:
time: 28.3 us; the launch traced here: 28.2 us
  Pallas kernels  26.9 us (95%)
  between operations  0.64 us (2%)
  local copies, waits for them, and re-layouts  0.61 us (2%)
    pallas_call x1, Pallas kernels, local(): pl.pallas_call(functools.partial(kernel, n), out_shape=pltpu.VMEM((2 * ow...  26.9 us
    slice x1, local copies, waits for them, and re-layouts, local(): return (both[:own], both[own:])  0.61 us

profile of v4, /device:TPU:0, one launch (start us, length us, event | category | flops | bytes accessed | tf_op | source)
XLA Modules:
  0.0 28.2 jit_solution(13466241933864275011)
XLA Ops:
  0.6 26.9 %shard_map.95 = f32[64,128]{1,0:T(8,128)S(1)} custom-call(f32[32,128]{1,0:T(8,128)} %forcing_in.1, f32[32,128]{1,0:T(8,128)} %guess_in.1, s32[3,8192]{1,0:T(4,128)} %corners_in.1, f32[4,8192]{1,0:T(4,128)} %gradients_in.1, f32[64,128]{1,0:T(8,128)} %bitcast.2, f32[64,128]{1,0:T(8,128)} %bitcast.3, s32[1,4,8]{2,1,0:T(4,128)} %send_in.1, s32[1,4,8]{2,1,0:T(4,128)} %recv_in.1), custom_call_target="tpu_custom_call" | custom-call | tf_op jit(solution)/shard_map/pallas_call | solution.py:643
  27.5 0.6 %fusion = (f32[32,128]{1,0:T(8,128)}, f32[32,128]{1,0:T(8,128)}) fusion(f32[64,128]{1,0:T(8,128)S(1)} %shard_map.95), kind=kLoop, calls=%fused_computation | loop fusion | bytes 65536 | tf_op jit(solution)/shard_map/slice | solution.py:704

commit v5 on v4

--- a/solution.py
+++ b/solution.py
@@ -11,6 +11,8 @@
 ROWS = 8
 HEAT = 6
 PARTS = 2
+FIRST = (1, 2)
+LATER = ((1,), ())
 PUSH = 8
 
 
@@ -284,19 +286,24 @@
         hi[here, :] = jnp.where(block < own, 1.0, -1.0)
         lane[here, :] = lax.bitwise_and(node, LANES - 1)
 
-    tall = lax.broadcasted_iota(jnp.int32, (LANES, LANES), 0)
+    tall = lax.broadcasted_iota(jnp.int32, (LANES, LANES), 0).astype(f32).astype(bf16)
 
     def heat(g, carry):
         for j in range(HEAT * ROWS):
             at = g * (HEAT * ROWS) + j
-            code = jnp.where(lane[pl.ds(at, 1), :] == tall, hi[pl.ds(at, 1), :], 0.0)
-            code = code.astype(bf16)
+
+            def filled(ref):
+                row = jnp.broadcast_to(ref[pl.ds(at, 1), :].astype(f32), (2 * ROWS, LANES))
+                return jnp.concatenate([row.astype(bf16)] * (LANES // (2 * ROWS)), axis=0)
+
+            code = jnp.where(filled(lane) == tall, filled(hi), jnp.zeros((LANES, LANES), bf16))
             block, row = divmod(j, ROWS)
-            if block % 3 == 1:
+            if block % 3 > 0:
                 column = (g * (HEAT // 3) + block // 3) * ROWS + row
                 columns = pl.ds(pl.multiple_of(column * LANES, LANES), LANES)
-                wide_hot[0:LANES, columns] = jnp.maximum(code, 0.0).astype(hot.dtype)
-                wide_hot[LANES : 2 * LANES, columns] = jnp.maximum(-code, 0.0).astype(hot.dtype)
+                side = block % 3 - 1
+                wide_hot[side, 0:LANES, columns] = jnp.maximum(code, 0.0).astype(hot.dtype)
+                wide_hot[side, LANES : 2 * LANES, columns] = jnp.maximum(-code, 0.0).astype(hot.dtype)
             code = code.T
             to = pl.ds(pl.multiple_of(at * LANES, LANES), LANES)
             hot[to, 0:LANES] = jnp.maximum(code, 0.0).astype(hot.dtype)
@@ -330,16 +337,16 @@
                 value = jnp.where(block == b, got, value)
             return value
 
-        def multiplied(g):
+        def multiplied(c, g):
             columns = pl.ds(pl.multiple_of(g * (ROWS * LANES), ROWS * LANES), ROWS * LANES)
             product = lax.dot_general(
                 split[...],
-                wide_hot[:, columns],
+                wide_hot[c - 1, :, columns],
                 (((1,), (0,)), ((), ())),
                 preferred_element_type=f32,
             )
             product = product[:wide_rows] + product[wide_rows:]
-            at = pl.multiple_of((g * 3 + 1) * ROWS, ROWS)
+            at = pl.multiple_of((g * 3 + c) * ROWS, ROWS)
             rows_left = []
             for j in range(ROWS):
                 kept = jnp.where(
@@ -359,8 +366,10 @@
                 bit *= 2
             return rows_left[0]
 
-        def spread(g, energy):
-            u = [picked(0, g, own), multiplied(g), picked(2, g, nodes)]
+        def spread(g, energy, products):
+            u = [picked(0, g, own)] + [
+                multiplied(c, g) if c in products else picked(c, g, nodes) for c in (1, 2)
+            ]
             if t > 0:
                 for c in range(3):
                     vals[t - 1, at_corner(c, g), :] = u[c]
@@ -395,7 +404,7 @@
         bounds = [-(-groups * i // PARTS) for i in range(PARTS + 1)]
         energy = jnp.zeros((ROWS, LANES), f32)
         for g in range(bounds[0], bounds[1]):
-            energy = spread(g, energy)
+            energy = spread(g, energy, FIRST)
         sums = jnp.zeros((2 * wide_rows, 2 * LANES), f32)
         for part in range(1, PARTS):
 
@@ -403,13 +412,15 @@
                 sums, energy = carry
                 sums = summed(bounds[part - 1], bounds[part], sums)
                 for g in range(bounds[part], bounds[part + 1]):
-                    energy = spread(g, energy)
+                    energy = spread(g, energy, LATER[(g - bounds[part]) % len(LATER)])
                 return sums, energy
 
             sums, energy = lax.fori_loop(0, once, step, (sums, energy))
         if gathered is not None:
             gathered()
-        sums = summed(bounds[PARTS - 1], groups, sums)
+        sums = lax.fori_loop(
+            0, once, lambda _, sums: summed(bounds[PARTS - 1], groups, sums), sums
+        )
         sums = sums[:wide_rows] + sums[wide_rows:]
         return sums[:own, :LANES], sums[:halo, LANES:], energy
 
@@ -659,7 +670,7 @@
             pltpu.VMEM((3 * rows, LANES), jnp.int32),
             pltpu.VMEM((3 * rows, LANES), jnp.int32),
             pltpu.VMEM((3 * count, 2 * LANES), jnp.float8_e4m3fn),
-            pltpu.VMEM((2 * LANES, count), jnp.float8_e4m3fn),
+            pltpu.VMEM((2, 2 * LANES, count), jnp.float8_e4m3fn),
             pltpu.VMEM((2 * own, 2 * LANES), jnp.bfloat16),
             pltpu.VMEM((4 * rows, LANES), f32),
             pltpu.VMEM((2, 3 * rows, LANES), f32),

time: 28.3 us -> 27.7 us (0.979)
  Pallas kernels: 26.9 us -> 26.3 us
    pallas_call x1, Pallas kernels: 26.9 us -> 26.3 us  [local(): pl.pallas_call(functools.partial(kernel, n), out_shape=pltpu.VMEM((2 * ow...]
where the time goes in v5:
time: 27.7 us; the launch traced here: 27.6 us
  Pallas kernels  26.3 us (95%)
  between operations  0.64 us (2%)
  local copies, waits for them, and re-layouts  0.61 us (2%)
    pallas_call x1, Pallas kernels, local(): pl.pallas_call(functools.partial(kernel, n), out_shape=pltpu.VMEM((2 * ow...  26.3 us
    slice x1, local copies, waits for them, and re-layouts, local(): return (both[:own], both[own:])  0.61 us

profile of v5, /device:TPU:0, one launch (start us, length us, event | category | flops | bytes accessed | tf_op | source)
XLA Modules:
  0.0 27.6 jit_solution(8650539588747494441)
XLA Ops:
  0.6 26.3 %shard_map.95 = f32[64,128]{1,0:T(8,128)S(1)} custom-call(f32[32,128]{1,0:T(8,128)} %forcing_in.1, f32[32,128]{1,0:T(8,128)} %guess_in.1, s32[3,8192]{1,0:T(4,128)} %corners_in.1, f32[4,8192]{1,0:T(4,128)} %gradients_in.1, f32[64,128]{1,0:T(8,128)} %bitcast.2, f32[64,128]{1,0:T(8,128)} %bitcast.3, s32[1,4,8]{2,1,0:T(4,128)} %send_in.1, s32[1,4,8]{2,1,0:T(4,128)} %recv_in.1), custom_call_target="tpu_custom_call" | custom-call | tf_op jit(solution)/shard_map/pallas_call | solution.py:654
  26.9 0.6 %fusion = (f32[32,128]{1,0:T(8,128)}, f32[32,128]{1,0:T(8,128)}) fusion(f32[64,128]{1,0:T(8,128)S(1)} %shard_map.95), kind=kLoop, calls=%fused_computation | loop fusion | bytes 65536 | tf_op jit(solution)/shard_map/slice | solution.py:715

commit v6 on v5

--- a/solution.py
+++ b/solution.py
@@ -323,6 +323,17 @@
     def at_corner(c, g):
         return pl.ds(pl.multiple_of((g * 3 + c) * ROWS, ROWS), ROWS)
 
+    small = lax.broadcasted_iota(jnp.int32, (1, LANES), 1)
+
+    def whole(a):
+        return jnp.sum(jnp.sum(a, axis=0, keepdims=True), axis=1, keepdims=True)
+
+    def packed(terms):
+        line = jnp.zeros((1, LANES), f32)
+        for i, term in enumerate(terms):
+            line = jnp.where(small == i, whole(term), line)
+        return line
+
     sublane = lax.broadcasted_iota(jnp.int32, (ROWS, LANES), 0)
     once = 1 + jnp.minimum(me, 0)
 
@@ -410,19 +421,27 @@
 
             def step(_, carry, part=part):
                 sums, energy = carry
-                sums = summed(bounds[part - 1], bounds[part], sums)
+                if gathered is None:
+                    sums = summed(bounds[part - 1], bounds[part], sums)
                 for g in range(bounds[part], bounds[part + 1]):
-                    energy = spread(g, energy, LATER[(g - bounds[part]) % len(LATER)])
+                    products = FIRST if gathered else LATER[(g - bounds[part]) % len(LATER)]
+                    energy = spread(g, energy, products)
                 return sums, energy
 
             sums, energy = lax.fori_loop(0, once, step, (sums, energy))
         if gathered is not None:
             gathered()
-        sums = lax.fori_loop(
-            0, once, lambda _, sums: summed(bounds[PARTS - 1], groups, sums), sums
-        )
+        first = bounds[PARTS - 1] if gathered is None else 0
+
+        def finish(_, carry):
+            sums, line = carry
+            if t == 1:
+                line = packed([table[t, 0:own] * table[t, 0:own], energy])
+            return summed(first, groups, sums), line
+
+        sums, line = lax.fori_loop(0, once, finish, (sums, jnp.zeros((1, LANES), f32)))
         sums = sums[:wide_rows] + sums[wide_rows:]
-        return sums[:own, :LANES], sums[:halo, LANES:], energy
+        return sums[:own, :LANES], sums[:halo, LANES:], line
 
     def element(g, u, with_energy):
         gx0, gy0, gx1, gy1 = [
@@ -507,15 +526,7 @@
         table[t, own:nodes] = halo_total
         divide(own_total, halo_total)
 
-    small = lax.broadcasted_iota(jnp.int32, (1, LANES), 1)
-
-    def whole(a):
-        return jnp.sum(jnp.sum(a, axis=0, keepdims=True), axis=1, keepdims=True)
-
-    def start_sum(k, terms):
-        line = jnp.zeros((1, LANES), f32)
-        for i, term in enumerate(terms):
-            line = jnp.where(small == i, whole(term), line)
+    def start_sum(k, line):
         sum_out[k] = line
         sum_in[k, me] = line
 
@@ -542,8 +553,7 @@
             for ahead in range(first + steps * PUSH, last):
                 push(ahead)
 
-        push_some(n // 2, n)
-        push_some(1, n // 2)
+        push_some(1, n)
 
     def sum_bytes(k):
         return sum_in.at[k, pl.ds(0, n - 1)]
@@ -568,10 +578,9 @@
     for i in range(3, len(rounds) + 1):
         next_round(i)
 
-    own_part, halo_part, energy = operate(1)
+    own_part, halo_part, line = operate(1)
     exchange(1, own_part, halo_part)
-    residual = table[1, 0:own]
-    start_sum(0, [residual * residual, energy])
+    start_sum(0, line)
     own_total, halo_total = collect(1, own_part, halo_part)
     fill(2, own_total, halo_total)
 
@@ -594,7 +603,7 @@
         for g in range(groups):
             energy = pair_energy(g, energy)
         later = residual - step * image
-        start_sum(1, [later * later, energy, later * image])
+        start_sum(1, packed([later * later, energy, later * image]))
 
     own_part, halo_part, _ = operate(2, second_sums)
     for o in range(offsets):
@@ -616,10 +625,12 @@
     for e in range(2):
         for i, distance in enumerate(distances):
             when_there(distance, lambda e=e, i=i: mix_copy(e, i).wait_send())
+    moved = guess[...] + step * residual
+    per_norm = 1.0 / norm
     fresh, own_pair, mixed = finish_sum(1, 3)
-    beta = fresh / norm
+    beta = fresh * per_norm
     next_step = fresh / (own_pair + beta * (2.0 * mixed + beta * crossed))
-    both[0:own] = guess[...] + step * residual + next_step * (later + beta * residual)
+    both[0:own] = moved + next_step * (later + beta * residual)
     both[own : 2 * own] = later - next_step * (applied + beta * image)
     for k in range(2):
         pltpu.make_async_copy(sum_bytes(k), sum_bytes(k), sum_send_sem.at[k]).wait()

time: 27.7 us -> 27.4 us (0.989)
  Pallas kernels: 26.3 us -> 26 us
    pallas_call x1, Pallas kernels: 26.3 us -> 26 us  [local(): pl.pallas_call(functools.partial(kernel, n), out_shape=pltpu.VMEM((2 * ow...]
where the time goes in v6:
time: 27.4 us; the launch traced here: 27.3 us
  Pallas kernels  26 us (95%)
  between operations  0.64 us (2%)
  local copies, waits for them, and re-layouts  0.61 us (2%)
    pallas_call x1, Pallas kernels, local(): pl.pallas_call(functools.partial(kernel, n), out_shape=pltpu.VMEM((2 * ow...  26 us
    slice x1, local copies, waits for them, and re-layouts, local(): return (both[:own], both[own:])  0.61 us

profile of v6, /device:TPU:0, one launch (start us, length us, event | category | flops | bytes accessed | tf_op | source)
XLA Modules:
  0.0 27.3 jit_solution(2171900710250737880)
XLA Ops:
  0.6 26.0 %shard_map.95 = f32[64,128]{1,0:T(8,128)S(1)} custom-call(f32[32,128]{1,0:T(8,128)} %forcing_in.1, f32[32,128]{1,0:T(8,128)} %guess_in.1, s32[3,8192]{1,0:T(4,128)} %corners_in.1, f32[4,8192]{1,0:T(4,128)} %gradients_in.1, f32[64,128]{1,0:T(8,128)} %bitcast.2, f32[64,128]{1,0:T(8,128)} %bitcast.3, s32[1,4,8]{2,1,0:T(4,128)} %send_in.1, s32[1,4,8]{2,1,0:T(4,128)} %recv_in.1), custom_call_target="tpu_custom_call" | custom-call | tf_op jit(solution)/shard_map/pallas_call | solution.py:665
  26.6 0.6 %fusion = (f32[32,128]{1,0:T(8,128)}, f32[32,128]{1,0:T(8,128)}) fusion(f32[64,128]{1,0:T(8,128)S(1)} %shard_map.95), kind=kLoop, calls=%fused_computation | loop fusion | bytes 65536 | tf_op jit(solution)/shard_map/slice | solution.py:726

commit v7 on v6

--- a/solution.py
+++ b/solution.py
@@ -13,6 +13,7 @@
 PARTS = 2
 FIRST = (1, 2)
 LATER = ((1,), ())
+LAST = ((1, 2), (1, 2), (1,))
 PUSH = 8
 
 
@@ -105,7 +106,6 @@
     shifts = shift_list(offsets)
     pairs = message_pairs(shifts)
     distances = list(pairs)
-    reach = max(distances)
     order = sorted(distances, key=lambda distance: (-abs(distance), distance))
     me = lax.axis_index("dom")
     f32 = jnp.float32
@@ -173,10 +173,9 @@
             ]
         )
     ]
-    for load in loads[:3]:
-        load.start()
     barrier = pltpu.get_barrier_semaphore()
-    for distance in distances:
+    near = max(shifts)
+    for distance in shifts:
         when_there(
             distance,
             lambda distance=distance: pl.semaphore_signal(
@@ -187,9 +186,9 @@
             ),
         )
 
-    for load in loads[3:]:
+    for load in loads:
         load.start()
-    rounds = learning_rounds(n, reach)
+    rounds = learning_rounds(n, near)
 
     def tell(i):
         for side in range(2):
@@ -229,7 +228,7 @@
                 (1, LANES), send[0, o, s], jnp.int32
             )
     pl.semaphore_wait(
-        barrier, jnp.minimum(me, reach) + jnp.minimum(n - 1 - me, reach)
+        barrier, jnp.minimum(me, near) + jnp.minimum(n - 1 - me, near)
     )
     for o in range(offsets):
         when_there(-shifts[o], lambda o=o: guess_copy(o).start())
@@ -337,7 +336,7 @@
     sublane = lax.broadcasted_iota(jnp.int32, (ROWS, LANES), 0)
     once = 1 + jnp.minimum(me, 0)
 
-    def operate(t, gathered=None):
+    def operate(t, step=None, gathered=None):
         def picked(c, g, count):
             index = lane[at_corner(c, g), :]
             block = blk[at_corner(c, g), :]
@@ -381,15 +380,19 @@
             u = [picked(0, g, own)] + [
                 multiplied(c, g) if c in products else picked(c, g, nodes) for c in (1, 2)
             ]
-            if t > 0:
-                for c in range(3):
-                    vals[t - 1, at_corner(c, g), :] = u[c]
             adds, local_energy = element(g, u, t == 1)
+            for c in range(3):
+                if t == 1:
+                    vals[at_corner(c, g), :] = u[c]
+                if t == 2:
+                    u[c] = vals[at_corner(c, g), :] - step * u[c]
+            if t == 2:
+                local_energy = element(g, u, True)[1]
             for c in range(3):
                 top = adds[c].astype(bf16).astype(f32)
                 hi[at_corner(c, g), :] = top
                 lo[at_corner(c, g), :] = adds[c] - top
-            return energy + local_energy if t == 1 else energy
+            return energy + local_energy if t > 0 else energy
 
         def summed(first, last, sums):
             parts = []
@@ -414,23 +417,24 @@
 
         bounds = [-(-groups * i // PARTS) for i in range(PARTS + 1)]
         energy = jnp.zeros((ROWS, LANES), f32)
-        for g in range(bounds[0], bounds[1]):
-            energy = spread(g, energy, FIRST)
         sums = jnp.zeros((2 * wide_rows, 2 * LANES), f32)
-        for part in range(1, PARTS):
-
-            def step(_, carry, part=part):
-                sums, energy = carry
-                if gathered is None:
+        if gathered is not None:
+            for g in range(groups):
+                energy = spread(g, energy, LAST[g % len(LAST)])
+            gathered(energy)
+        else:
+            for g in range(bounds[0], bounds[1]):
+                energy = spread(g, energy, FIRST)
+            for part in range(1, PARTS):
+
+                def some(_, carry, part=part):
+                    sums, energy = carry
                     sums = summed(bounds[part - 1], bounds[part], sums)
-                for g in range(bounds[part], bounds[part + 1]):
-                    products = FIRST if gathered else LATER[(g - bounds[part]) % len(LATER)]
-                    energy = spread(g, energy, products)
-                return sums, energy
-
-            sums, energy = lax.fori_loop(0, once, step, (sums, energy))
-        if gathered is not None:
-            gathered()
+                    for g in range(bounds[part], bounds[part + 1]):
+                        energy = spread(g, energy, LATER[(g - bounds[part]) % len(LATER)])
+                    return sums, energy
+
+                sums, energy = lax.fori_loop(0, once, some, (sums, energy))
         first = bounds[PARTS - 1] if gathered is None else 0
 
         def finish(_, carry):
@@ -575,42 +579,30 @@
         when_there(shifts[o], lambda o=o: link_copy(o).wait_recv())
     own_total, halo_total = collect(0, own_part, halo_part)
     fill(1, own_total, halo_total)
-    for i in range(3, len(rounds) + 1):
-        next_round(i)
+    next_round(3)
 
     own_part, halo_part, line = operate(1)
     exchange(1, own_part, halo_part)
+    for i in range(4, len(rounds) + 1):
+        next_round(i)
     start_sum(0, line)
     own_total, halo_total = collect(1, own_part, halo_part)
     fill(2, own_total, halo_total)
 
-    residual, image = table[1, 0:own], table[2, 0:own]
-    scalars = []
-
-    def second_sums():
-        norm, crossed = finish_sum(0, 2)
-        step = norm / crossed
-        scalars.extend([norm, crossed, step])
-
-        def pair_energy(g, energy):
-            u = [
-                vals[0, at_corner(c, g), :] - step * vals[1, at_corner(c, g), :]
-                for c in range(3)
-            ]
-            return energy + element(g, u, True)[1]
-
-        energy = jnp.zeros((ROWS, LANES), f32)
-        for g in range(groups):
-            energy = pair_energy(g, energy)
+    norm, crossed = finish_sum(0, 2)
+    step = norm / crossed
+
+    def second_sums(energy):
+        residual, image = table[1, 0:own], table[2, 0:own]
         later = residual - step * image
         start_sum(1, packed([later * later, energy, later * image]))
 
-    own_part, halo_part, _ = operate(2, second_sums)
+    own_part, halo_part, _ = operate(2, step, second_sums)
     for o in range(offsets):
         back_out[o] = halo_part[o * slots : (o + 1) * slots]
     for o in range(offsets):
         when_there(shifts[o], lambda o=o: back_copy(o).start())
-    norm, crossed, step = scalars
+    residual, image = table[1, 0:own], table[2, 0:own]
     later = residual - step * image
 
     for o in range(offsets):
@@ -684,7 +676,7 @@
             pltpu.VMEM((2, 2 * LANES, count), jnp.float8_e4m3fn),
             pltpu.VMEM((2 * own, 2 * LANES), jnp.bfloat16),
             pltpu.VMEM((4 * rows, LANES), f32),
-            pltpu.VMEM((2, 3 * rows, LANES), f32),
+            pltpu.VMEM((3 * rows, LANES), f32),
             pltpu.VMEM((3 * rows, LANES), f32),
             pltpu.VMEM((3 * rows, LANES), f32),
             pltpu.VMEM((3, nodes, LANES), f32),
@@ -708,7 +700,7 @@
             dma((offsets,)),
             dma((2,)),
             dma((2,)),
-            pltpu.SemaphoreType.REGULAR((len(learning_rounds(n, max(pairs))) + 1, 2)),
+            pltpu.SemaphoreType.REGULAR((len(learning_rounds(n, max(shift_list(offsets)))) + 1, 2)),
         ],
         compiler_params=pltpu.CompilerParams(
             collective_id=0, has_side_effects=True

time: 27.4 us -> 27.4 us (level)
  no operation moved by 1% of the time
where the time goes in v7:
time: 27.4 us; the launch traced here: 27.2 us
  Pallas kernels  26 us (95%)
  between operations  0.64 us (2%)
  local copies, waits for them, and re-layouts  0.61 us (2%)
    pallas_call x1, Pallas kernels, local(): pl.pallas_call(functools.partial(kernel, n), out_shape=pltpu.VMEM((2 * ow...  26 us
    slice x1, local copies, waits for them, and re-layouts, local(): return (both[:own], both[own:])  0.61 us

profile of v7, /device:TPU:0, one launch (start us, length us, event | category | flops | bytes accessed | tf_op | source)
XLA Modules:
  0.0 27.2 jit_solution(13371936322686379848)
XLA Ops:
  0.6 26.0 %shard_map.95 = f32[64,128]{1,0:T(8,128)S(1)} custom-call(f32[32,128]{1,0:T(8,128)} %forcing_in.1, f32[32,128]{1,0:T(8,128)} %guess_in.1, s32[3,8192]{1,0:T(4,128)} %corners_in.1, f32[4,8192]{1,0:T(4,128)} %gradients_in.1, f32[64,128]{1,0:T(8,128)} %bitcast.2, f32[64,128]{1,0:T(8,128)} %bitcast.3, s32[1,4,8]{2,1,0:T(4,128)} %send_in.1, s32[1,4,8]{2,1,0:T(4,128)} %recv_in.1), custom_call_target="tpu_custom_call" | custom-call | tf_op jit(solution)/shard_map/pallas_call | solution.py:657
  26.6 0.6 %fusion = (f32[32,128]{1,0:T(8,128)}, f32[32,128]{1,0:T(8,128)}) fusion(f32[64,128]{1,0:T(8,128)S(1)} %shard_map.95), kind=kLoop, calls=%fused_computation | loop fusion | bytes 65536 | tf_op jit(solution)/shard_map/slice | solution.py:718

commit v8 on v7

--- a/solution.py
+++ b/solution.py
@@ -336,7 +336,7 @@
     sublane = lax.broadcasted_iota(jnp.int32, (ROWS, LANES), 0)
     once = 1 + jnp.minimum(me, 0)
 
-    def operate(t, step=None, gathered=None):
+    def operate(t, length=None, gathered=None):
         def picked(c, g, count):
             index = lane[at_corner(c, g), :]
             block = blk[at_corner(c, g), :]
@@ -376,23 +376,22 @@
                 bit *= 2
             return rows_left[0]
 
-        def spread(g, energy, products):
+        def spread(g, energy, products, step=None):
             u = [picked(0, g, own)] + [
                 multiplied(c, g) if c in products else picked(c, g, nodes) for c in (1, 2)
             ]
             adds, local_energy = element(g, u, t == 1)
-            for c in range(3):
-                if t == 1:
-                    vals[at_corner(c, g), :] = u[c]
-                if t == 2:
-                    u[c] = vals[at_corner(c, g), :] - step * u[c]
-            if t == 2:
+            if t == 1 or t == 2 and step is None:
+                for c in range(3):
+                    vals[t - 1, at_corner(c, g), :] = u[c]
+            if step is not None:
+                u = [vals[0, at_corner(c, g), :] - step * u[c] for c in range(3)]
                 local_energy = element(g, u, True)[1]
             for c in range(3):
                 top = adds[c].astype(bf16).astype(f32)
                 hi[at_corner(c, g), :] = top
                 lo[at_corner(c, g), :] = adds[c] - top
-            return energy + local_energy if t > 0 else energy
+            return energy if local_energy is None else energy + local_energy
 
         def summed(first, last, sums):
             parts = []
@@ -419,9 +418,18 @@
         energy = jnp.zeros((ROWS, LANES), f32)
         sums = jnp.zeros((2 * wide_rows, 2 * LANES), f32)
         if gathered is not None:
-            for g in range(groups):
+            for g in range(groups // 2):
                 energy = spread(g, energy, LAST[g % len(LAST)])
-            gathered(energy)
+            step = length()
+            for g in range(groups // 2):
+                u = [
+                    vals[0, at_corner(c, g), :] - step * vals[1, at_corner(c, g), :]
+                    for c in range(3)
+                ]
+                energy = energy + element(g, u, True)[1]
+            for g in range(groups // 2, groups):
+                energy = spread(g, energy, LAST[g % len(LAST)], step)
+            gathered(energy, step)
         else:
             for g in range(bounds[0], bounds[1]):
                 energy = spread(g, energy, FIRST)
@@ -589,15 +597,20 @@
     own_total, halo_total = collect(1, own_part, halo_part)
     fill(2, own_total, halo_total)
 
-    norm, crossed = finish_sum(0, 2)
-    step = norm / crossed
-
-    def second_sums(energy):
+    scalars = []
+
+    def step_length():
+        norm, crossed = finish_sum(0, 2)
+        scalars.extend([norm, crossed, norm / crossed])
+        return scalars[2]
+
+    def second_sums(energy, step):
         residual, image = table[1, 0:own], table[2, 0:own]
         later = residual - step * image
         start_sum(1, packed([later * later, energy, later * image]))
 
-    own_part, halo_part, _ = operate(2, step, second_sums)
+    own_part, halo_part, _ = operate(2, step_length, second_sums)
+    norm, crossed, step = scalars
     for o in range(offsets):
         back_out[o] = halo_part[o * slots : (o + 1) * slots]
     for o in range(offsets):
@@ -676,7 +689,7 @@
             pltpu.VMEM((2, 2 * LANES, count), jnp.float8_e4m3fn),
             pltpu.VMEM((2 * own, 2 * LANES), jnp.bfloat16),
             pltpu.VMEM((4 * rows, LANES), f32),
-            pltpu.VMEM((3 * rows, LANES), f32),
+            pltpu.VMEM((2, 3 * rows, LANES), f32),
             pltpu.VMEM((3 * rows, LANES), f32),
             pltpu.VMEM((3 * rows, LANES), f32),
             pltpu.VMEM((3, nodes, LANES), f32),

time: 27.4 us -> 27.2 us (level)
  no operation moved by 1% of the time
where the time goes in v8:
time: 27.2 us; the launch traced here: 27.1 us
  Pallas kernels  25.8 us (95%)
  between operations  0.64 us (2%)
  local copies, waits for them, and re-layouts  0.61 us (2%)
    pallas_call x1, Pallas kernels, local(): pl.pallas_call(functools.partial(kernel, n), out_shape=pltpu.VMEM((2 * ow...  25.8 us
    slice x1, local copies, waits for them, and re-layouts, local(): return (both[:own], both[own:])  0.61 us

profile of v8, /device:TPU:0, one launch (start us, length us, event | category | flops | bytes accessed | tf_op | source)
XLA Modules:
  0.0 27.1 jit_solution(14987641525468260521)
XLA Ops:
  0.6 25.8 %shard_map.95 = f32[64,128]{1,0:T(8,128)S(1)} custom-call(f32[32,128]{1,0:T(8,128)} %forcing_in.1, f32[32,128]{1,0:T(8,128)} %guess_in.1, s32[3,8192]{1,0:T(4,128)} %corners_in.1, f32[4,8192]{1,0:T(4,128)} %gradients_in.1, f32[64,128]{1,0:T(8,128)} %bitcast.2, f32[64,128]{1,0:T(8,128)} %bitcast.3, s32[1,4,8]{2,1,0:T(4,128)} %send_in.1, s32[1,4,8]{2,1,0:T(4,128)} %recv_in.1), custom_call_target="tpu_custom_call" | custom-call | tf_op jit(solution)/shard_map/pallas_call | solution.py:670
  26.5 0.6 %fusion = (f32[32,128]{1,0:T(8,128)}, f32[32,128]{1,0:T(8,128)}) fusion(f32[64,128]{1,0:T(8,128)S(1)} %shard_map.95), kind=kLoop, calls=%fused_computation | loop fusion | bytes 65536 | tf_op jit(solution)/shard_map/slice | solution.py:731
